TPU v7x, 256 devices: a whole 4x4x8 slice. The times are simulated.
256 devices in a mesh: dp: 4 (over y_hi, core), seq: 64 (over z, x, y_lo).
Axes of the slice: x: 4, y: 4 (y_hi: 2, y_lo: 2; y = y_hi * 2 + y_lo), z: 8, core: 2. Of those that a mesh axis runs over, the one named last changes fastest.
Arguments:
- queries: bfloat16 [4, 8192, 2048], P('dp', 'seq'), may hold values from -12 to 12
- keys: bfloat16 [4, 8192, 512], P('dp', 'seq'), may hold values from -4 to 4
- values: bfloat16 [4, 8192, 512], P('dp', 'seq'), may hold values from -6 to 6
- segments: int32 [4, 8192], P('dp', 'seq'), may hold values from 0 to 3, never falling along the last dimension, each value on 1 to 7168 neighbouring positions
- task_ids: int32 [4], replicated, may hold values from 0 to 127
- prompt_keys: bfloat16 [128, 128, 512], P('seq'), may hold values from -4 to 4
- prompt_values: bfloat16 [128, 128, 512], P('seq'), may hold values from -6 to 6
- grad_out: bfloat16 [4, 8192, 2048], P('dp', 'seq'), may hold values from -6 to 6
Outputs:
- attended: bfloat16 [4, 8192, 2048], P('dp', 'seq')
- prompt_key_grad: float32 [128, 128, 512], P('seq')
- prompt_value_grad: float32 [128, 128, 512], P('seq')
Inputs may be any that keep to these rules, and one draw needn't show every extreme that they name: `segments`: along each example the document numbers never fall; one document holds 7168 tokens.
All inputs are finite; a program needn't handle non-finite values.
Results may differ from a plain program's by a relative error of at most 0.0096.
Values may be sent and summed in bfloat16 or wider, within the bound.
No kernel may reach another device: no remote copies, remote signals or barrier semaphores. Data moves between devices by JAX's collectives and lax.ppermute only.
A program may use at most 128 MiB of HBM per device.

v0:
```python
import math

import jax
import jax.numpy as jnp
from jax import lax
from jax.experimental import pallas as pl
from jax.experimental.pallas import tpu as pltpu
from jax.sharding import Mesh
from jax.sharding import PartitionSpec as P

KVH = 4
GROUP = 4
HD = 128
PROMPT = 128
TOK = 128
WIDE = GROUP * HD
ZS = 8
CHUNK = 272
SEQ = ("zh", "zl", "x", "y")
ALL = ("dp", "zh", "zl", "x", "y")
SCALE = 1.0 / math.sqrt(HD)
LOG2E = math.log2(math.e)
FACTOR = SCALE * LOG2E
HIDDEN = -1e30
SPLIT = 2


ORDER = [(0, 0), (1, 0), (0, -1), (0, 1), (0, 2), (1, -1), (1, 1), (1, 2)]

VMEM = pl.BlockSpec(memory_space=pltpu.VMEM)
SMEM = pl.BlockSpec(memory_space=pltpu.SMEM)


HBM = pl.BlockSpec(memory_space=pltpu.HBM)


def params(mib=24):
    return pltpu.CompilerParams(vmem_limit_bytes=mib * 1024 * 1024)


def dot_nt(a, b):
    return lax.dot_general(a, b, (((1,), (1,)), ((), ())), preferred_element_type=jnp.float32)


def dot_tn(a, b):
    return lax.dot_general(a, b, (((0,), (0,)), ((), ())), preferred_element_type=jnp.float32)


def dot_nn(a, b):
    return lax.dot_general(a, b, (((1,), (0,)), ((), ())), preferred_element_type=jnp.float32)


def stacked_heads(block):
    return jnp.concatenate([block[:, g * HD : (g + 1) * HD] for g in range(GROUP)], axis=0)


def keys_kernel(keys_ref, values_ref, segments_ref, out_ref, seg_ref, sems):
    copies = [pltpu.make_async_copy(segments_ref, seg_ref, sems.at[0])]
    for z in range(ZS):
        cols = pl.ds(z // 2 * HD, HD)
        for n, source in enumerate((keys_ref, values_ref)):
            target = out_ref.at[z, pl.ds(n * TOK, TOK), :]
            copies.append(
                pltpu.make_async_copy(source.at[0, :, cols], target, sems.at[1 + 2 * z + n])
            )
    for copy in copies:
        copy.start()
    copies[0].wait()
    seg = seg_ref[...].astype(jnp.float32).astype(jnp.bfloat16)
    for z in range(ZS):
        out_ref[z, 2 * TOK : CHUNK, :] = jnp.broadcast_to(seg, (CHUNK - 2 * TOK, TOK))
    for copy in copies[1:]:
        copy.wait()


def keys_payload(keys, values, segments):
    return pl.pallas_call(
        keys_kernel,
        out_shape=jax.ShapeDtypeStruct((ZS, CHUNK, HD), jnp.bfloat16),
        in_specs=[HBM, HBM, HBM],
        out_specs=VMEM,
        scratch_shapes=[
            pltpu.VMEM((1, TOK), jnp.int32),
            pltpu.SemaphoreType.DMA((1 + 2 * ZS,)),
        ],
        compiler_params=params(),
        name="keys_payload",
    )(keys, values, segments)


def rows_kernel(tasks_ref, queries_ref, go_ref, pk_ref, pv_ref, *rest):
    outs, sems = rest[: 3 * KVH], rest[3 * KVH]
    slot = tasks_ref[lax.axis_index("dp")] % 2
    zh = lax.axis_index("zh")
    half = PROMPT // 2
    copies = []

    def add(source, target):
        copies.append(pltpu.make_async_copy(source, target, sems.at[len(copies)]))

    for d in range(KVH):
        h = (zh + d) % KVH
        cols = pl.ds(pl.multiple_of(h * WIDE, WIDE), WIDE)
        q_out, go_out, prompt_out = outs[d], outs[KVH + d], outs[2 * KVH + d]
        add(queries_ref.at[0, :, cols], q_out)
        own = pl.ds(pl.multiple_of(h * HD, HD), HD)
        for n, bank in enumerate((pk_ref, pv_ref)):
            for s in range(2):
                place = pl.ds((2 * n + s) * HD, HD)
                add(
                    bank.at[slot, pl.ds(s * half, half), own],
                    prompt_out.at[:, place],
                )
        add(go_ref.at[0, :, cols], go_out)
    for copy in copies:
        copy.start()
    for copy in copies:
        copy.wait()


def rows_payload(tasks, queries, go, prompt_keys, prompt_values):
    outs = pl.pallas_call(
        rows_kernel,
        out_shape=[jax.ShapeDtypeStruct((TOK, WIDE), jnp.bfloat16)] * (2 * KVH)
        + [jax.ShapeDtypeStruct((PROMPT // 2, WIDE), jnp.bfloat16)] * KVH,
        in_specs=[SMEM, HBM, HBM, HBM, HBM],
        out_specs=[VMEM] * (3 * KVH),
        scratch_shapes=[pltpu.SemaphoreType.DMA((6 * KVH,))],
        compiler_params=params(),
        name="rows_payload",
    )(tasks, queries, go, prompt_keys, prompt_values)
    return outs[:KVH], outs[KVH : 2 * KVH], outs[2 * KVH :]


class Bundle:
    def __init__(self, ref):
        self.ref = ref

    def keys(self, z):
        return self.ref[z, 0:TOK, :]

    def values(self, z):
        return self.ref[z, TOK : 2 * TOK, :]

    def segments(self, z):
        return self.ref[z, 2 * TOK : CHUNK, :].astype(jnp.float32)[0:1]


def accumulate(scores, wide, acc_ref, peak_ref, rows):
    old = peak_ref[rows]
    peak = jnp.maximum(old, jnp.max(scores, axis=1, keepdims=True))
    weights = jnp.exp2((scores - peak) * FACTOR).astype(jnp.bfloat16)
    shrink = jnp.exp2((old - peak) * FACTOR)
    acc_ref[rows] = acc_ref[rows] * shrink + dot_nn(weights, wide)
    peak_ref[rows] = peak


def absorb(bundles, j, q, seg_q, diagonal, acc_ref, peak_ref):
    zl, x, y = (lax.axis_index(name) for name in ("zl", "x", "y"))
    count = len(bundles) * 2 * TOK
    keys, values, visible = [], [], []
    for e in range(2):
        z = 2 * j + e
        for n, part in bundles.items():
            keys.append(part.keys(z))
            values.append(part.values(z))
            seg = part.segments(z)
            if diagonal and n != 0:
                b, c = ORDER[n]
                before = ((x + c + 4) % 4 * 2 + (y + b) % 2) < x * 2 + y
                shown = (zl > e) | ((zl == e) & before)
                seg = jnp.where(shown, seg, -1.0)
            same = seg_q == seg
            if diagonal and n == 0:
                reach = jnp.where(zl == e, 0, jnp.where(zl > e, TOK, -TOK))
                rows = lax.broadcasted_iota(jnp.int32, (TOK, TOK), 0)
                cols = lax.broadcasted_iota(jnp.int32, (TOK, TOK), 1)
                same = same & (cols - rows <= reach)
            visible.append(same)
    keys = jnp.concatenate(keys, axis=0)
    values = jnp.concatenate(values, axis=0)
    visible = jnp.concatenate(visible, axis=1)[None]
    wide = jnp.concatenate([values, jnp.ones(values.shape, jnp.bfloat16)], axis=1)
    size = GROUP * TOK // SPLIT
    scores = []
    for g in range(SPLIT):
        part = dot_nt(q[g * size : (g + 1) * size], keys).reshape(size // TOK, TOK, count)
        scores.append(jnp.where(visible, part, HIDDEN).reshape(size, count))
    for g in range(SPLIT):
        rows = slice(g * size, (g + 1) * size)
        accumulate(scores[g], wide, acc_ref, peak_ref, rows)


def sweep(bundles, own_ref, q, k, acc_ref, peak_ref):
    seg = own_ref[2 * k + lax.axis_index("zl"), 2 * TOK :, :].astype(jnp.float32)[0:1]
    seg_q = jnp.transpose(jnp.broadcast_to(seg, (TOK, TOK)))
    absorb(bundles, k, q, seg_q, True, acc_ref, peak_ref)

    def earlier(j, carry):
        absorb(bundles, j, q, seg_q, False, acc_ref, peak_ref)
        return carry

    lax.fori_loop(0, k, earlier, 0)


def first_kernel(names, *refs):
    q_refs, refs = refs[:KVH], refs[KVH:]
    bundles = {n: Bundle(ref) for n, ref in zip(names, refs)}
    refs = refs[len(names) :]
    out_ref, q_ref, state_ref, acc_ref, peak_ref, sems = refs
    own_ref = bundles[0].ref
    zh = lax.axis_index("zh")
    for d in range(KVH):
        q_ref[d] = stacked_heads(q_refs[d][...])

    def saved(d):
        return pltpu.make_async_copy(state_ref.at[d], out_ref.at[d], sems.at[d])

    def per_block(d, carry):
        acc_ref[...] = jnp.zeros_like(acc_ref)
        peak_ref[...] = jnp.full_like(peak_ref, HIDDEN)
        sweep(bundles, own_ref, q_ref[d], (zh - d + KVH) % KVH, acc_ref, peak_ref)
        state_ref[d, :, :HD] = acc_ref[:, :HD]
        lanes = lax.broadcasted_iota(jnp.int32, (GROUP * TOK, HD), 1)
        state_ref[d, :, HD:] = jnp.where(lanes < HD // 2, acc_ref[:, HD:], peak_ref[...])
        saved(d).start()
        return carry

    lax.fori_loop(0, KVH, per_block, 0)
    for d in range(KVH):
        saved(d).wait()


STATE = (KVH, GROUP * TOK, 2 * HD)


def cost(count):
    work = GROUP * TOK * HD * 4 * count * 2 * TOK * 10
    return pl.CostEstimate(flops=work, transcendentals=work // 512, bytes_accessed=1 << 22)


def attend_first(names, q, arrays):
    return pl.pallas_call(
        lambda *refs: first_kernel(names, *refs),
        out_shape=jax.ShapeDtypeStruct(STATE, jnp.float32),
        in_specs=[VMEM] * (KVH + len(arrays)),
        out_specs=pl.BlockSpec(memory_space=pltpu.HBM),
        scratch_shapes=[
            pltpu.VMEM((KVH, GROUP * TOK, HD), jnp.bfloat16),
            pltpu.VMEM(STATE, jnp.float32),
            pltpu.VMEM((GROUP * TOK, 2 * HD), jnp.float32),
            pltpu.VMEM((GROUP * TOK, 1), jnp.float32),
            pltpu.SemaphoreType.DMA((KVH,)),
        ],
        compiler_params=params(),
        cost_estimate=cost(len(names)),
        name="attend_first",
    )(*q, *arrays)


def last_kernel(names, *refs):
    q_refs, go_refs, refs = refs[:KVH], refs[KVH : 2 * KVH], refs[2 * KVH :]
    in_ref, own_ref, prompt_ref, *refs = refs
    bundles = {n: Bundle(ref) for n, ref in zip(names, refs)}
    refs = refs[len(names) :]
    att_refs, refs = refs[:KVH], refs[KVH:]
    grads_ref, q_ref, go_ref, state_ref, acc_ref, peak_ref, sums_ref, sems = refs
    zh = lax.axis_index("zh")

    def loaded(d):
        return pltpu.make_async_copy(in_ref.at[d], state_ref.at[d], sems.at[d])

    for d in range(KVH):
        loaded(d).start()
    for d in range(KVH):
        q_ref[d] = stacked_heads(q_refs[d][...])
        go_ref[d] = stacked_heads(go_refs[d][...])
    prompt_k = jnp.concatenate([prompt_ref[:, 0:HD], prompt_ref[:, HD : 2 * HD]], axis=0)
    prompt_v = jnp.concatenate([prompt_ref[:, 2 * HD : 3 * HD], prompt_ref[:, 3 * HD :]], axis=0)
    ones = jnp.ones(prompt_v.shape, jnp.bfloat16)
    prompt_wide = jnp.concatenate([prompt_v, ones], axis=1)
    sums_ref[...] = jnp.zeros_like(sums_ref)

    def per_block(d, carry):
        loaded(d).wait()
        q = q_ref[d]
        acc_ref[:, :HD] = state_ref[d, :, :HD]
        acc_ref[:, HD:] = jnp.broadcast_to(state_ref[d, :, HD : HD + 1], (GROUP * TOK, HD))
        peak_ref[...] = state_ref[d, :, 2 * HD - 1 :]
        accumulate(dot_nt(q, prompt_k), prompt_wide, acc_ref, peak_ref, slice(None))
        sweep(bundles, own_ref, q, (zh - d + KVH) % KVH, acc_ref, peak_ref)
        norm = acc_ref[:, HD:]
        attended = (acc_ref[:, :HD] / norm).astype(jnp.bfloat16)
        for n in range(KVH):

            @pl.when(d == n)
            def _():
                for g in range(GROUP):
                    att_refs[n][:, g * HD : (g + 1) * HD] = attended[g * TOK : (g + 1) * TOK]

        go = go_ref[d]
        delta = jnp.sum(
            go.astype(jnp.float32) * attended.astype(jnp.float32), axis=1, keepdims=True
        )
        log_norm = peak_ref[...] * FACTOR + jnp.log2(norm)
        probs = jnp.exp2(dot_nt(q, prompt_k) * FACTOR - log_norm)
        score_grad = probs * (dot_nt(go, prompt_v) - delta)
        sums_ref[0:PROMPT, :] += dot_tn(score_grad.astype(jnp.bfloat16), q) * SCALE
        sums_ref[PROMPT:, :] += dot_tn(probs.astype(jnp.bfloat16), go)
        return carry

    lax.fori_loop(0, KVH, per_block, 0)
    grads_ref[...] = sums_ref[...].astype(jnp.bfloat16)


def attend_last(names, q, go, state, own, prompt, arrays):
    outs = pl.pallas_call(
        lambda *refs: last_kernel(names, *refs),
        out_shape=[jax.ShapeDtypeStruct((TOK, WIDE), jnp.bfloat16)] * KVH
        + [jax.ShapeDtypeStruct((2 * PROMPT, HD), jnp.bfloat16)],
        in_specs=[VMEM] * (2 * KVH)
        + [pl.BlockSpec(memory_space=pltpu.HBM)]
        + [VMEM] * (2 + len(arrays)),
        out_specs=[VMEM] * (KVH + 1),
        scratch_shapes=[
            pltpu.VMEM((KVH, GROUP * TOK, HD), jnp.bfloat16),
            pltpu.VMEM((KVH, GROUP * TOK, HD), jnp.bfloat16),
            pltpu.VMEM(STATE, jnp.float32),
            pltpu.VMEM((GROUP * TOK, 2 * HD), jnp.float32),
            pltpu.VMEM((GROUP * TOK, 1), jnp.float32),
            pltpu.VMEM((2 * PROMPT, HD), jnp.float32),
            pltpu.SemaphoreType.DMA((KVH,)),
        ],
        compiler_params=params(),
        cost_estimate=cost(len(names) + 1),
        name="attend_last",
    )(*q, *go, state, own, prompt, *arrays)
    return outs[:KVH], outs[KVH]


def sum_kernel(pieces_ref, out_ref):
    total = pieces_ref[0].astype(jnp.float32)
    for r in range(1, 8):
        total += pieces_ref[r].astype(jnp.float32)
    for r in range(8):
        out_ref[r] = total.astype(jnp.bfloat16)


def summed(pieces):
    return pl.pallas_call(
        sum_kernel,
        out_shape=jax.ShapeDtypeStruct((8, 32, HD), jnp.bfloat16),
        in_specs=[VMEM],
        out_specs=VMEM,
        compiler_params=params(),
        name="summed",
    )(pieces)


def pairs_kernel(sent_ref, out_ref):
    for h in range(KVH):
        total = sent_ref[2 * h].astype(jnp.float32) + sent_ref[2 * h + 1].astype(jnp.float32)
        out_ref[h] = total.astype(jnp.bfloat16)


def pairs_summed(sent):
    return pl.pallas_call(
        pairs_kernel,
        out_shape=jax.ShapeDtypeStruct((KVH, 32, HD), jnp.bfloat16),
        in_specs=[VMEM],
        out_specs=VMEM,
        compiler_params=params(),
        name="pairs_summed",
    )(sent)


def route_kernel(tasks_ref, *refs):
    parts, out_ref = refs[:4], refs[4]
    dp = lax.axis_index("dp")
    first = (lax.axis_index("zh") * 2 + lax.axis_index("zl")) * 16
    tasks = [tasks_ref[dp ^ d] for d in range(4)]
    for h in range(KVH):
        examples = [part[h].astype(jnp.float32) for part in parts]
        for r in range(8):
            for j in range(2):
                total = jnp.zeros(examples[0].shape, jnp.float32)
                for d in range(4):
                    total += jnp.where(tasks[d] == first + r * 2 + j, examples[d], 0.0)
                out_ref[r, j, h] = total.astype(jnp.bfloat16)


def route(tasks, parts):
    return pl.pallas_call(
        route_kernel,
        out_shape=jax.ShapeDtypeStruct((8, 2, KVH, 32, HD), jnp.bfloat16),
        in_specs=[SMEM] + [VMEM] * 4,
        out_specs=VMEM,
        compiler_params=params(),
        name="route",
    )(tasks, *parts)


def banks_kernel(banks_ref, key_ref, value_ref):
    for r in range(8):
        out_ref = key_ref if r < 4 else value_ref
        rows = slice(r % 4 * 32, r % 4 * 32 + 32)
        for j in range(2):
            for h in range(KVH):
                out_ref[j, rows, h * HD : (h + 1) * HD] = banks_ref[r, j, h].astype(jnp.float32)


def banks_out(banks):
    shape = jax.ShapeDtypeStruct((2, PROMPT, KVH * HD), jnp.float32)
    return pl.pallas_call(
        banks_kernel,
        out_shape=(shape, shape),
        compiler_params=params(),
        name="banks_out",
    )(banks)


def heads_kernel(*refs):
    out_ref = refs[KVH]
    zh = lax.axis_index("zh")
    for d in range(KVH):
        h = (zh + d) % KVH
        out_ref[0, :, pl.ds(pl.multiple_of(h * WIDE, WIDE), WIDE)] = refs[d][...]


def heads_out(parts):
    return pl.pallas_call(
        heads_kernel,
        out_shape=jax.ShapeDtypeStruct((1, TOK, KVH * WIDE), jnp.bfloat16),
        compiler_params=params(),
        name="heads_out",
    )(*parts)


def swap(value, axis):
    return lax.ppermute(value, axis, [(0, 1), (1, 0)])


def from_left(value):
    return lax.ppermute(value, "x", [(i, (i + 1) % 4) for i in range(4)])


def from_right(value):
    return lax.ppermute(value, "x", [(i, (i - 1) % 4) for i in range(4)])


def crosswise(value, step):
    pairs = [(x * 2 + y, (x + step) % 4 * 2 + 1 - y) for x in range(4) for y in range(2)]
    return lax.ppermute(value, ("x", "y"), pairs)


def turned(parts, sign):
    moved = [parts[0]]
    for d in range(1, KVH):
        moved.append(
            lax.ppermute(parts[d], "zh", [(i, (i + sign * d) % 4) for i in range(4)])
        )
    return moved


def exchange(blocks, axes):
    return lax.all_to_all(blocks, axes, 0, 0, tiled=True)


def choose(index, own, others):
    chosen = own
    for position, other in others:
        chosen = jnp.where(index == position, other, chosen)
    return chosen


def step(queries, keys, values, segments, task_ids, prompt_keys, prompt_values, grad_out):
    dp, zh, zl, x, y = (lax.axis_index(name) for name in ALL)
    owner = task_ids[dp] // 2
    own_zh, own_zl, own_x, own_y = owner // 16, (owner // 8) % 2, (owner // 2) % 4, owner % 2

    payload = keys_payload(keys, values, segments)
    own = exchange(payload, ("zh", "zl"))
    q, go, prompts = rows_payload(
        task_ids, queries, grad_out, prompt_keys, prompt_values
    )
    prompts = turned(prompts, 1)

    beside = swap(own, "y")
    left = from_left(own)
    right = from_right(own)
    q = turned(q, 1)
    across = from_left(left)
    beside_across = crosswise(right, -1)
    beside_left = from_left(beside)
    beside_right = from_right(beside)
    go = turned(go, 1)

    prompt = choose((zh - own_zh) % KVH, prompts[0], list(enumerate(prompts))[1:])
    flip_zl, flip_y = (own_zl != zl).astype(jnp.int32), (own_y != y).astype(jnp.int32)
    both = lax.ppermute(prompt, ("zl", "y"), [(i, 3 - i) for i in range(4)])
    flipped = swap(prompt, "zl")
    beyond = swap(prompt, "y")
    prompt = choose(flip_zl * 2 + flip_y, prompt, [(2, flipped), (1, beyond), (3, both)])
    far = lax.ppermute(prompt, "x", [(i, (i + 2) % 4) for i in range(4)])
    sides = [((x + 3) % 4, from_left(prompt))]
    sides.append(((x + 1) % 4, from_right(prompt)))
    prompt = choose(own_x, prompt, sides + [((x + 2) % 4, far)])

    state = attend_first((0, 1, 2, 3), q, (own, beside, left, right))
    attended, grads = attend_last(
        (4, 5, 6, 7),
        q,
        go,
        state,
        own,
        prompt,
        (across, beside_left, beside_right, beside_across),
    )

    attended = turned(attended, -1)
    pieces = exchange(grads.reshape(8, 32, HD), ("x", "y"))
    sent = exchange(summed(pieces), ("zh", "zl"))
    mine = pairs_summed(sent)
    parts = [mine]
    for d in range(1, 4):
        parts.append(lax.ppermute(mine, "dp", [(i, i ^ d) for i in range(4)]))
    routed = route(task_ids, parts)
    banks = exchange(routed, ("x", "y"))
    key_grad, value_grad = banks_out(banks)
    return heads_out(attended), key_grad, value_grad


def solution(mesh):
    split = Mesh(mesh.devices.reshape(4, 4, 2, 4, 2), ALL)
    return jax.shard_map(
        step,
        mesh=split,
        in_specs=(
            P("dp", SEQ, None),
            P("dp", SEQ, None),
            P("dp", SEQ, None),
            P("dp", SEQ),
            P(),
            P(SEQ, None, None),
            P(SEQ, None, None),
            P("dp", SEQ, None),
        ),
        out_specs=(P("dp", SEQ, None), P(SEQ, None, None), P(SEQ, None, None)),
        check_vma=False,
    )
```

profile of v0, /device:TPU:2, one launch (start us, length us, event | category | flops | bytes accessed | tf_op | source)
XLA Modules:
  0.0 204.7 jit_solution(9735744069687275298)
XLA Ops:
  3.2 1.1 keys_payload.1
  4.3 8.5 %all-to-all-start = ((bf16[8,272,128]{2,1,0:T(8,128)(2,1)}), bf16[8,272,128]{2,1,0:T(8,128)(2,1)S(1)}, u32[]{:S(2)}, u32[]{:S(2)}) async-start(bf16[8,272,128]{2,1,0:T(8,128)(2,1)} %keys_payload.1), calls=%async_computation | async-start | bytes 1114112 | tf_op jit(solution)/shard_map/all_to_all | solution.py:466
  16.5 5.9 %collective-permute-start.10 = (bf16[64,512]{1,0:T(8,128)(2,1)S(1)}, bf16[64,512]{1,0:T(8,128)(2,1)S(1)}, u32[]{:S(2)}, u32[]{:S(2)}) collective-permute-start(bf16[64,512]{1,0:T(8,128)(2,1)S(1)} %get-tuple-element.31), channel_id=1, source_target_pairs={{0,32},{16,48},{32,0},{48,16},{1,33},{17,49},{33,1},{49,17},{2,34}... | collective-permute-start | bytes 196616 | tf_op jit(solution)/shard_map/ppermute | solution.py:460
  23.0 3.6 %collective-permute-start.9 = (bf16[64,512]{1,0:T(8,128)(2,1)S(1)}, bf16[64,512]{1,0:T(8,128)(2,1)S(1)}, u32[]{:S(2)}, u32[]{:S(2)}) collective-permute-start(bf16[64,512]{1,0:T(8,128)(2,1)S(1)} %get-tuple-element.30), channel_id=1, source_target_pairs={{0,48},{16,0},{32,16},{48,32},{1,49},{17,1},{33,17},{49,33},{2,50}... | collective-permute-start | bytes 196616 | tf_op jit(solution)/shard_map/ppermute | solution.py:460
  29.8 4.7 %collective-permute-done.10 = bf16[64,512]{1,0:T(8,128)(2,1)S(1)} collective-permute-done((bf16[64,512]{1,0:T(8,128)(2,1)S(1)}, bf16[64,512]{1,0:T(8,128)(2,1)S(1)}, u32[]{:S(2)}, u32[]{:S(2)}) %collective-permute-start.10) | collective-permute-done | bytes 65568 | tf_op jit(solution)/shard_map/ppermute | solution.py:460
  35.5 2.6 %collective-permute-start.12 = (bf16[64,512]{1,0:T(8,128)(2,1)}, bf16[64,512]{1,0:T(8,128)(2,1)}, u32[]{:S(2)}, u32[]{:S(2)}) collective-permute-start(bf16[64,512]{1,0:T(8,128)(2,1)} %select_select_fusion.2), channel_id=1, source_target_pairs={{0,9},{1,8},{8,1},{9,0},{2,11},{3,10},{10,3},{11,2},{4,13},{5,12},... | collective-permute-start | bytes 196616 | tf_op jit(solution)/shard_map/ppermute | solution.py:500
  38.6 1.5 collective-permute-start.7
  40.6 1.6 collective-permute-start.13
  42.7 10.1 %collective-permute-done.13 = bf16[64,512]{1,0:T(8,128)(2,1)S(1)} collective-permute-done((bf16[64,512]{1,0:T(8,128)(2,1)}, bf16[64,512]{1,0:T(8,128)(2,1)S(1)}, u32[]{:S(2)}, u32[]{:S(2)}) %collective-permute-start.13) | collective-permute-done | bytes 65568 | tf_op jit(solution)/shard_map/ppermute | solution.py:440
  53.4 1.8 collective-permute-start
  55.8 2.7 %collective-permute-start.1 = (bf16[128,512]{1,0:T(8,128)(2,1)S(1)}, bf16[128,512]{1,0:T(8,128)(2,1)S(1)}, u32[]{:S(2)}, u32[]{:S(2)}) collective-permute-start(bf16[128,512]{1,0:T(8,128)(2,1)S(1)} %get-tuple-element.24), channel_id=1, source_target_pairs={{0,32},{16,48},{32,0},{48,16},{1,33},{17,49},{33,1},{49,17},{2,34}... | collective-permute-start | bytes 393224 | tf_op jit(solution)/shard_map/ppermute | solution.py:460
  58.5 5.9 %collective-permute-done.refs_1_ = bf16[128,512]{1,0:T(8,128)(2,1)S(1)} collective-permute-done((bf16[128,512]{1,0:T(8,128)(2,1)S(1)}, bf16[128,512]{1,0:T(8,128)(2,1)S(1)}, u32[]{:S(2)}, u32[]{:S(2)}) %collective-permute-start) | collective-permute-done | bytes 131104 | tf_op jit(solution)/shard_map/ppermute | solution.py:460
  64.4 2.2 %collective-permute-start.2 = (bf16[128,512]{1,0:T(8,128)(2,1)S(1)}, bf16[128,512]{1,0:T(8,128)(2,1)S(1)}, u32[]{:S(2)}, u32[]{:S(2)}) collective-permute-start(bf16[128,512]{1,0:T(8,128)(2,1)S(1)} %get-tuple-element.25), channel_id=1, source_target_pairs={{0,48},{16,0},{32,16},{48,32},{1,49},{17,1},{33,17},{49,33},{2,50}... | collective-permute-start | bytes 393224 | tf_op jit(solution)/shard_map/ppermute | solution.py:460
  66.6 2.1 %collective-permute-done.1.refs_2_ = bf16[128,512]{1,0:T(8,128)(2,1)S(1)} collective-permute-done((bf16[128,512]{1,0:T(8,128)(2,1)S(1)}, bf16[128,512]{1,0:T(8,128)(2,1)S(1)}, u32[]{:S(2)}, u32[]{:S(2)}) %collective-permute-start.1) | collective-permute-done | bytes 131104 | tf_op jit(solution)/shard_map/ppermute | solution.py:460
  69.6 1.3 collective-permute-done.2.refs_3_
  70.9 2.1 %collective-permute-start.15 = (bf16[64,512]{1,0:T(8,128)(2,1)S(1)}, bf16[64,512]{1,0:T(8,128)(2,1)}, u32[]{:S(2)}, u32[]{:S(2)}) collective-permute-start(bf16[64,512]{1,0:T(8,128)(2,1)S(1)} %select_select_fusion.1), channel_id=1, source_target_pairs={{0,4},{2,6},{4,0},{6,2},{1,5},{3,7},{5,1},{7,3},{8,12},{10,14},{12... | collective-permute-start | bytes 196616 | tf_op jit(solution)/shard_map/ppermute | solution.py:504
  73.1 3.7 %collective-permute-done.3.refs_5_ = bf16[128,512]{1,0:T(8,128)(2,1)S(1)} collective-permute-done((bf16[128,512]{1,0:T(8,128)(2,1)S(1)}, bf16[128,512]{1,0:T(8,128)(2,1)S(1)}, u32[]{:S(2)}, u32[]{:S(2)}) %collective-permute-start.3) | collective-permute-done | bytes 131104 | tf_op jit(solution)/shard_map/ppermute | solution.py:460
  77.3 1.5 collective-permute-start.19
  78.8 1.5 collective-permute-start.20
  80.8 4.3 %collective-permute-start.21 = (bf16[8,272,128]{2,1,0:T(8,128)(2,1)S(1)}, bf16[8,272,128]{2,1,0:T(8,128)(2,1)}, u32[]{:S(2)}, u32[]{:S(2)}) collective-permute-start(bf16[8,272,128]{2,1,0:T(8,128)(2,1)S(1)} %collective-permute-done.8.refs_7_), channel_id=1, source_target_pairs={{0,7},{1,6},{2,1},{3,0},{4,3},{5,2},{6,5},{7,4},{8,15},{9,14},{10,... | collective-permute-start | bytes 1671176 | tf_op jit(solution)/shard_map/ppermute | solution.py:453
  85.1 20.5 %collective-permute-done.17 = bf16[64,512]{1,0:T(8,128)(2,1)} collective-permute-done((bf16[64,512]{1,0:T(8,128)(2,1)S(1)}, bf16[64,512]{1,0:T(8,128)(2,1)}, u32[]{:S(2)}, u32[]{:S(2)}) %collective-permute-start.17) | collective-permute-done | bytes 65568 | tf_op jit(solution)/shard_map/ppermute | solution.py:444
  106.5 9.9 %collective-permute-done.4.refs_6_ = bf16[128,512]{1,0:T(8,128)(2,1)S(1)} collective-permute-done((bf16[128,512]{1,0:T(8,128)(2,1)}, bf16[128,512]{1,0:T(8,128)(2,1)S(1)}, u32[]{:S(2)}, u32[]{:S(2)}) %collective-permute-start.4) | collective-permute-done | bytes 131104 | tf_op jit(solution)/shard_map/ppermute | solution.py:460
  116.5 11.6 %attend_first.1.refs_8_ = f32[4,512,256]{2,1,0:T(8,128)S(1)} custom-call(bf16[128,512]{1,0:T(8,128)(2,1)S(1)} %get-tuple-element.22.refs_0_, bf16[128,512]{1,0:T(8,128)(2,1)S(1)} %collective-permute-done.refs_1_, bf16[128,512]{1,0:T(8,128)(2,1)S(1)} %collective-permute-done.1.refs_2_, bf16[128,512]{1,0:T(8,128)(2,1)S(1)} %collective-permute-done.2.refs_3_, ...), custom_call_target="tpu_custom_call" | custom-call | flops 2684354560 | bytes 4194304 | tf_op jit(solution)/shard_map/attend_first/pallas_call | solution.py:243
  128.2 19.1 %attend_last.1 = (bf16[128,512]{1,0:T(8,128)(2,1)S(1)}, bf16[128,512]{1,0:T(8,128)(2,1)S(1)}, bf16[128,512]{1,0:T(8,128)(2,1)S(1)}, bf16[128,512]{1,0:T(8,128)(2,1)S(1)}, bf16[256,128]{1,0:T(8,128)(2,1)S(1)}) custom-call(bf16[128,512]{1,0:T(8,128)(2,1)S(1)} %get-tuple-element.22.refs_0_, bf16[128,512]{1,0:T(8,128)(2,1)S(1)} %collective-permute-done.refs_1_, ...), custom_call_target="tpu_custom_call" | custom-call | flops 3355443200 | bytes 4194304 | tf_op jit(solution)/shard_map/attend_last/pallas_call | solution.py:317
  147.3 8.7 %all_to_all.20.pieces_ref = bf16[8,32,128]{2,1,0:T(8,128)(2,1)S(1)} all-to-all(bf16[8,32,128]{2,1,0:T(8,128)(2,1)S(1)} %bitcast.2), channel_id=1, replica_groups=mesh['dp'=4,'zh'=4,'zl'=2,'x'=4,'y'=2] {'x','y'}, dimensions={0} | all-to-all | bytes 131072 | tf_op jit(solution)/shard_map/all_to_all | solution.py:466
  156.0 19.3 %all_to_all.21.sent_ref = bf16[8,32,128]{2,1,0:T(8,128)(2,1)S(1)} all-to-all(bf16[8,32,128]{2,1,0:T(8,128)(2,1)S(1)} %summed.1), channel_id=1, replica_groups=mesh['dp'=4,'zh'=4,'zl'=2,'x'=4,'y'=2] {'zh','zl'}, dimensions={0} | all-to-all | bytes 131072 | tf_op jit(solution)/shard_map/all_to_all | solution.py:466
  175.5 3.3 %collective-permute-start.27 = (bf16[4,32,128]{2,1,0:T(8,128)(2,1)S(1)}, bf16[4,32,128]{2,1,0:T(8,128)(2,1)S(1)}, u32[]{:S(2)}, u32[]{:S(2)}) collective-permute-start(bf16[4,32,128]{2,1,0:T(8,128)(2,1)S(1)} %pairs_summed.1.refs_0_), channel_id=1, source_target_pairs={{0,192},{64,128},{128,64},{192,0},{1,193},{65,129},{129,65},{193,1... | collective-permute-start | bytes 98312 | tf_op jit(solution)/shard_map/ppermute | solution.py:526
  178.8 2.3 %collective-permute-done.26.refs_2_ = bf16[4,32,128]{2,1,0:T(8,128)(2,1)S(1)} collective-permute-done((bf16[4,32,128]{2,1,0:T(8,128)(2,1)S(1)}, bf16[4,32,128]{2,1,0:T(8,128)(2,1)S(1)}, u32[]{:S(2)}, u32[]{:S(2)}) %collective-permute-start.26) | collective-permute-done | bytes 32800 | tf_op jit(solution)/shard_map/ppermute | solution.py:526
  181.1 1.7 route.1
  182.7 4.9 %all-to-all-start.3 = ((bf16[8,2,4,32,128]{4,3,2,1,0:T(8,128)(2,1)}), bf16[8,2,4,32,128]{4,3,2,1,0:T(8,128)(2,1)S(1)}, u32[]{:S(2)}, u32[]{:S(2)}) async-start(bf16[8,2,4,32,128]{4,3,2,1,0:T(8,128)(2,1)} %route.1), calls=%async_computation.3 | async-start | bytes 1048576 | tf_op jit(solution)/shard_map/all_to_all | solution.py:466
  188.0 3.7 %collective-permute-start.23 = (bf16[128,512]{1,0:T(8,128)(2,1)S(1)}, bf16[128,512]{1,0:T(8,128)(2,1)S(1)}, u32[]{:S(2)}, u32[]{:S(2)}) collective-permute-start(bf16[128,512]{1,0:T(8,128)(2,1)S(1)} %get-tuple-element.36), channel_id=1, source_target_pairs={{0,32},{16,48},{32,0},{48,16},{1,33},{17,49},{33,1},{49,17},{2,34}... | collective-permute-start | bytes 393224 | tf_op jit(solution)/shard_map/ppermute | solution.py:460
  191.7 10.3 %collective-permute-done.22.refs_1_ = bf16[128,512]{1,0:T(8,128)(2,1)S(1)} collective-permute-done((bf16[128,512]{1,0:T(8,128)(2,1)S(1)}, bf16[128,512]{1,0:T(8,128)(2,1)S(1)}, u32[]{:S(2)}, u32[]{:S(2)}) %collective-permute-start.22) | collective-permute-done | bytes 131104 | tf_op jit(solution)/shard_map/ppermute | solution.py:460
  (73 shorter events, 17.5 us)
Async XLA Ops:
  0.6 12.2 %copy-start.2 = (bf16[2,128,512]{2,1,0:T(8,128)(2,1)S(1)}, bf16[2,128,512]{2,1,0:T(8,128)(2,1)}, u32[]{:S(2)}) copy-start(bf16[2,128,512]{2,1,0:T(8,128)(2,1)} %pk_ref.1) | copy-start | bytes 786436
  3.2 23.4 %copy-start.7 = (s32[4]{0:T(128)S(1)}, s32[4]{0:T(128)}, u32[]{:S(2)}) copy-start(s32[4]{0:T(128)} %tasks_ref.3) | copy-start | bytes 52
  4.3 33.8 %all-to-all-start = ((bf16[8,272,128]{2,1,0:T(8,128)(2,1)}), bf16[8,272,128]{2,1,0:T(8,128)(2,1)S(1)}, u32[]{:S(2)}, u32[]{:S(2)}) async-start(bf16[8,272,128]{2,1,0:T(8,128)(2,1)} %keys_payload.1), calls=%async_computation | async-start | bytes 1114112 | tf_op jit(solution)/shard_map/all_to_all | solution.py:466
  16.5 18.0 %collective-permute-start.10 = (bf16[64,512]{1,0:T(8,128)(2,1)S(1)}, bf16[64,512]{1,0:T(8,128)(2,1)S(1)}, u32[]{:S(2)}, u32[]{:S(2)}) collective-permute-start(bf16[64,512]{1,0:T(8,128)(2,1)S(1)} %get-tuple-element.31), channel_id=1, source_target_pairs={{0,32},{16,48},{32,0},{48,16},{1,33},{17,49},{33,1},{49,17},{2,34}... | collective-permute-start | bytes 196616 | tf_op jit(solution)/shard_map/ppermute | solution.py:460
  22.4 12.4 %collective-permute-start.11 = (bf16[64,512]{1,0:T(8,128)(2,1)S(1)}, bf16[64,512]{1,0:T(8,128)(2,1)S(1)}, u32[]{:S(2)}, u32[]{:S(2)}) collective-permute-start(bf16[64,512]{1,0:T(8,128)(2,1)S(1)} %get-tuple-element.32), channel_id=1, source_target_pairs={{0,16},{16,32},{32,48},{48,0},{1,17},{17,33},{33,49},{49,1},{2,18}... | collective-permute-start | bytes 196616 | tf_op jit(solution)/shard_map/ppermute | solution.py:460
  23.0 11.9 %collective-permute-start.9 = (bf16[64,512]{1,0:T(8,128)(2,1)S(1)}, bf16[64,512]{1,0:T(8,128)(2,1)S(1)}, u32[]{:S(2)}, u32[]{:S(2)}) collective-permute-start(bf16[64,512]{1,0:T(8,128)(2,1)S(1)} %get-tuple-element.30), channel_id=1, source_target_pairs={{0,48},{16,0},{32,16},{48,32},{1,49},{17,1},{33,17},{49,33},{2,50}... | collective-permute-start | bytes 196616 | tf_op jit(solution)/shard_map/ppermute | solution.py:460
  35.5 6.7 %collective-permute-start.12 = (bf16[64,512]{1,0:T(8,128)(2,1)}, bf16[64,512]{1,0:T(8,128)(2,1)}, u32[]{:S(2)}, u32[]{:S(2)}) collective-permute-start(bf16[64,512]{1,0:T(8,128)(2,1)} %select_select_fusion.2), channel_id=1, source_target_pairs={{0,9},{1,8},{8,1},{9,0},{2,11},{3,10},{10,3},{11,2},{4,13},{5,12},... | collective-permute-start | bytes 196616 | tf_op jit(solution)/shard_map/ppermute | solution.py:500
  38.1 39.2 %collective-permute-start.6 = (bf16[8,272,128]{2,1,0:T(8,128)(2,1)S(1)}, bf16[8,272,128]{2,1,0:T(8,128)(2,1)S(1)}, u32[]{:S(2)}, u32[]{:S(2)}) collective-permute-start(bf16[8,272,128]{2,1,0:T(8,128)(2,1)S(1)} %all-to-all-done.refs_4_.refs_9_), channel_id=1, source_target_pairs={{0,1},{1,0},{2,3},{3,2},{4,5},{5,4},{6,7},{7,6},{8,9},{9,8},{10,11... | collective-permute-start | bytes 1671176 | tf_op jit(solution)/shard_map/ppermute | solution.py:440
  38.6 41.8 %collective-permute-start.7 = (bf16[8,272,128]{2,1,0:T(8,128)(2,1)S(1)}, bf16[8,272,128]{2,1,0:T(8,128)(2,1)S(1)}, u32[]{:S(2)}, u32[]{:S(2)}) collective-permute-start(bf16[8,272,128]{2,1,0:T(8,128)(2,1)S(1)} %all-to-all-done.refs_4_.refs_9_), channel_id=1, source_target_pairs={{0,2},{2,4},{4,6},{6,0},{1,3},{3,5},{5,7},{7,1},{8,10},{10,12},{12... | collective-permute-start | bytes 1671176 | tf_op jit(solution)/shard_map/ppermute | solution.py:444
  40.1 40.8 %collective-permute-start.8 = (bf16[8,272,128]{2,1,0:T(8,128)(2,1)S(1)}, bf16[8,272,128]{2,1,0:T(8,128)(2,1)S(1)}, u32[]{:S(2)}, u32[]{:S(2)}) collective-permute-start(bf16[8,272,128]{2,1,0:T(8,128)(2,1)S(1)} %all-to-all-done.refs_4_.refs_9_), channel_id=1, source_target_pairs={{0,6},{2,0},{4,2},{6,4},{1,7},{3,1},{5,3},{7,5},{8,14},{10,8},{12,... | collective-permute-start | bytes 1671176 | tf_op jit(solution)/shard_map/ppermute | solution.py:448
  40.6 12.1 %collective-permute-start.13 = (bf16[64,512]{1,0:T(8,128)(2,1)}, bf16[64,512]{1,0:T(8,128)(2,1)S(1)}, u32[]{:S(2)}, u32[]{:S(2)}) collective-permute-start(bf16[64,512]{1,0:T(8,128)(2,1)} %select_select_fusion.2), channel_id=1, source_target_pairs={{0,1},{1,0},{2,3},{3,2},{4,5},{5,4},{6,7},{7,6},{8,9},{9,8},{10,11... | collective-permute-start | bytes 196616 | tf_op jit(solution)/shard_map/ppermute | solution.py:440
  42.2 13.0 %collective-permute-start.14 = (bf16[64,512]{1,0:T(8,128)(2,1)}, bf16[64,512]{1,0:T(8,128)(2,1)S(1)}, u32[]{:S(2)}, u32[]{:S(2)}) collective-permute-start(bf16[64,512]{1,0:T(8,128)(2,1)} %select_select_fusion.2), channel_id=1, source_target_pairs={{0,8},{8,0},{1,9},{9,1},{2,10},{10,2},{3,11},{11,3},{4,12},{12,4},... | collective-permute-start | bytes 196616 | tf_op jit(solution)/shard_map/ppermute | solution.py:440
  53.4 11.0 %collective-permute-start = (bf16[128,512]{1,0:T(8,128)(2,1)S(1)}, bf16[128,512]{1,0:T(8,128)(2,1)S(1)}, u32[]{:S(2)}, u32[]{:S(2)}) collective-permute-start(bf16[128,512]{1,0:T(8,128)(2,1)S(1)} %get-tuple-element.23), channel_id=1, source_target_pairs={{0,16},{16,32},{32,48},{48,0},{1,17},{17,33},{33,49},{49,1},{2,18}... | collective-permute-start | bytes 393224 | tf_op jit(solution)/shard_map/ppermute | solution.py:460
  55.8 12.8 %collective-permute-start.1 = (bf16[128,512]{1,0:T(8,128)(2,1)S(1)}, bf16[128,512]{1,0:T(8,128)(2,1)S(1)}, u32[]{:S(2)}, u32[]{:S(2)}) collective-permute-start(bf16[128,512]{1,0:T(8,128)(2,1)S(1)} %get-tuple-element.24), channel_id=1, source_target_pairs={{0,32},{16,48},{32,0},{48,16},{1,33},{17,49},{33,1},{49,17},{2,34}... | collective-permute-start | bytes 393224 | tf_op jit(solution)/shard_map/ppermute | solution.py:460
  64.4 6.5 %collective-permute-start.2 = (bf16[128,512]{1,0:T(8,128)(2,1)S(1)}, bf16[128,512]{1,0:T(8,128)(2,1)S(1)}, u32[]{:S(2)}, u32[]{:S(2)}) collective-permute-start(bf16[128,512]{1,0:T(8,128)(2,1)S(1)} %get-tuple-element.25), channel_id=1, source_target_pairs={{0,48},{16,0},{32,16},{48,32},{1,49},{17,1},{33,17},{49,33},{2,50}... | collective-permute-start | bytes 393224 | tf_op jit(solution)/shard_map/ppermute | solution.py:460
  68.7 8.1 %collective-permute-start.3 = (bf16[128,512]{1,0:T(8,128)(2,1)S(1)}, bf16[128,512]{1,0:T(8,128)(2,1)S(1)}, u32[]{:S(2)}, u32[]{:S(2)}) collective-permute-start(bf16[128,512]{1,0:T(8,128)(2,1)S(1)} %get-tuple-element.27), channel_id=1, source_target_pairs={{0,16},{16,32},{32,48},{48,0},{1,17},{17,33},{33,49},{49,1},{2,18}... | collective-permute-start | bytes 393224 | tf_op jit(solution)/shard_map/ppermute | solution.py:460
  70.9 7.9 %collective-permute-start.15 = (bf16[64,512]{1,0:T(8,128)(2,1)S(1)}, bf16[64,512]{1,0:T(8,128)(2,1)}, u32[]{:S(2)}, u32[]{:S(2)}) collective-permute-start(bf16[64,512]{1,0:T(8,128)(2,1)S(1)} %select_select_fusion.1), channel_id=1, source_target_pairs={{0,4},{2,6},{4,0},{6,2},{1,5},{3,7},{5,1},{7,3},{8,12},{10,14},{12... | collective-permute-start | bytes 196616 | tf_op jit(solution)/shard_map/ppermute | solution.py:504
  76.8 8.3 %collective-permute-start.16 = (bf16[64,512]{1,0:T(8,128)(2,1)S(1)}, bf16[64,512]{1,0:T(8,128)(2,1)}, u32[]{:S(2)}, u32[]{:S(2)}) collective-permute-start(bf16[64,512]{1,0:T(8,128)(2,1)S(1)} %select_select_fusion.1), channel_id=1, source_target_pairs={{0,6},{2,0},{4,2},{6,4},{1,7},{3,1},{5,3},{7,5},{8,14},{10,8},{12,... | collective-permute-start | bytes 196616 | tf_op jit(solution)/shard_map/ppermute | solution.py:448
  77.3 50.8 %collective-permute-start.19 = (bf16[8,272,128]{2,1,0:T(8,128)(2,1)S(1)}, bf16[8,272,128]{2,1,0:T(8,128)(2,1)S(1)}, u32[]{:S(2)}, u32[]{:S(2)}) collective-permute-start(bf16[8,272,128]{2,1,0:T(8,128)(2,1)S(1)} %collective-permute-done.6.refs_5_), channel_id=1, source_target_pairs={{0,2},{2,4},{4,6},{6,0},{1,3},{3,5},{5,7},{7,1},{8,10},{10,12},{12... | collective-permute-start | bytes 1671176 | tf_op jit(solution)/shard_map/ppermute | solution.py:444
  78.8 49.3 %collective-permute-start.20 = (bf16[8,272,128]{2,1,0:T(8,128)(2,1)S(1)}, bf16[8,272,128]{2,1,0:T(8,128)(2,1)}, u32[]{:S(2)}, u32[]{:S(2)}) collective-permute-start(bf16[8,272,128]{2,1,0:T(8,128)(2,1)S(1)} %collective-permute-done.6.refs_5_), channel_id=1, source_target_pairs={{0,6},{2,0},{4,2},{6,4},{1,7},{3,1},{5,3},{7,5},{8,14},{10,8},{12,... | collective-permute-start | bytes 1671176 | tf_op jit(solution)/shard_map/ppermute | solution.py:448
  80.3 47.8 %collective-permute-start.18 = (bf16[8,272,128]{2,1,0:T(8,128)(2,1)S(1)}, bf16[8,272,128]{2,1,0:T(8,128)(2,1)}, u32[]{:S(2)}, u32[]{:S(2)}) collective-permute-start(bf16[8,272,128]{2,1,0:T(8,128)(2,1)S(1)} %collective-permute-done.7.refs_6_), channel_id=1, source_target_pairs={{0,2},{2,4},{4,6},{6,0},{1,3},{3,5},{5,7},{7,1},{8,10},{10,12},{12... | collective-permute-start | bytes 1671176 | tf_op jit(solution)/shard_map/ppermute | solution.py:444
  80.8 47.3 %collective-permute-start.21 = (bf16[8,272,128]{2,1,0:T(8,128)(2,1)S(1)}, bf16[8,272,128]{2,1,0:T(8,128)(2,1)}, u32[]{:S(2)}, u32[]{:S(2)}) collective-permute-start(bf16[8,272,128]{2,1,0:T(8,128)(2,1)S(1)} %collective-permute-done.8.refs_7_), channel_id=1, source_target_pairs={{0,7},{1,6},{2,1},{3,0},{4,3},{5,2},{6,5},{7,4},{8,15},{9,14},{10,... | collective-permute-start | bytes 1671176 | tf_op jit(solution)/shard_map/ppermute | solution.py:453
  85.1 20.5 %collective-permute-start.17 = (bf16[64,512]{1,0:T(8,128)(2,1)S(1)}, bf16[64,512]{1,0:T(8,128)(2,1)}, u32[]{:S(2)}, u32[]{:S(2)}) collective-permute-start(bf16[64,512]{1,0:T(8,128)(2,1)S(1)} %select_select_fusion.1), channel_id=1, source_target_pairs={{0,2},{2,4},{4,6},{6,0},{1,3},{3,5},{5,7},{7,1},{8,10},{10,12},{12... | collective-permute-start | bytes 196616 | tf_op jit(solution)/shard_map/ppermute | solution.py:444
  105.6 10.8 %collective-permute-start.4 = (bf16[128,512]{1,0:T(8,128)(2,1)}, bf16[128,512]{1,0:T(8,128)(2,1)S(1)}, u32[]{:S(2)}, u32[]{:S(2)}) collective-permute-start(bf16[128,512]{1,0:T(8,128)(2,1)} %copy-done.12), channel_id=1, source_target_pairs={{0,32},{16,48},{32,0},{48,16},{1,33},{17,49},{33,1},{49,17},{2,34}... | collective-permute-start | bytes 393224 | tf_op jit(solution)/shard_map/ppermute | solution.py:460
  116.4 11.7 %collective-permute-start.5 = (bf16[128,512]{1,0:T(8,128)(2,1)}, bf16[128,512]{1,0:T(8,128)(2,1)S(1)}, u32[]{:S(2)}, u32[]{:S(2)}) collective-permute-start(bf16[128,512]{1,0:T(8,128)(2,1)} %copy-done.11), channel_id=1, source_target_pairs={{0,48},{16,0},{32,16},{48,32},{1,49},{17,1},{33,17},{49,33},{2,50}... | collective-permute-start | bytes 393224 | tf_op jit(solution)/shard_map/ppermute | solution.py:460
  175.3 3.5 %collective-permute-start.25 = (bf16[4,32,128]{2,1,0:T(8,128)(2,1)S(1)}, bf16[4,32,128]{2,1,0:T(8,128)(2,1)S(1)}, u32[]{:S(2)}, u32[]{:S(2)}) collective-permute-start(bf16[4,32,128]{2,1,0:T(8,128)(2,1)S(1)} %pairs_summed.1.refs_0_), channel_id=1, source_target_pairs={{0,64},{64,0},{128,192},{192,128},{1,65},{65,1},{129,193},{193,129... | collective-permute-start | bytes 98312 | tf_op jit(solution)/shard_map/ppermute | solution.py:526
  175.4 5.6 %collective-permute-start.26 = (bf16[4,32,128]{2,1,0:T(8,128)(2,1)S(1)}, bf16[4,32,128]{2,1,0:T(8,128)(2,1)S(1)}, u32[]{:S(2)}, u32[]{:S(2)}) collective-permute-start(bf16[4,32,128]{2,1,0:T(8,128)(2,1)S(1)} %pairs_summed.1.refs_0_), channel_id=1, source_target_pairs={{0,128},{64,192},{128,0},{192,64},{1,129},{65,193},{129,1},{193,65... | collective-permute-start | bytes 98312 | tf_op jit(solution)/shard_map/ppermute | solution.py:526
  175.5 5.6 %collective-permute-start.27 = (bf16[4,32,128]{2,1,0:T(8,128)(2,1)S(1)}, bf16[4,32,128]{2,1,0:T(8,128)(2,1)S(1)}, u32[]{:S(2)}, u32[]{:S(2)}) collective-permute-start(bf16[4,32,128]{2,1,0:T(8,128)(2,1)S(1)} %pairs_summed.1.refs_0_), channel_id=1, source_target_pairs={{0,192},{64,128},{128,64},{192,0},{1,193},{65,129},{129,65},{193,1... | collective-permute-start | bytes 98312 | tf_op jit(solution)/shard_map/ppermute | solution.py:526
  182.7 20.9 %all-to-all-start.3 = ((bf16[8,2,4,32,128]{4,3,2,1,0:T(8,128)(2,1)}), bf16[8,2,4,32,128]{4,3,2,1,0:T(8,128)(2,1)S(1)}, u32[]{:S(2)}, u32[]{:S(2)}) async-start(bf16[8,2,4,32,128]{4,3,2,1,0:T(8,128)(2,1)} %route.1), calls=%async_computation.3 | async-start | bytes 1048576 | tf_op jit(solution)/shard_map/all_to_all | solution.py:466
  187.6 14.4 %collective-permute-start.22 = (bf16[128,512]{1,0:T(8,128)(2,1)S(1)}, bf16[128,512]{1,0:T(8,128)(2,1)S(1)}, u32[]{:S(2)}, u32[]{:S(2)}) collective-permute-start(bf16[128,512]{1,0:T(8,128)(2,1)S(1)} %get-tuple-element.35), channel_id=1, source_target_pairs={{0,48},{16,0},{32,16},{48,32},{1,49},{17,1},{33,17},{49,33},{2,50}... | collective-permute-start | bytes 393224 | tf_op jit(solution)/shard_map/ppermute | solution.py:460
  188.0 14.0 %collective-permute-start.23 = (bf16[128,512]{1,0:T(8,128)(2,1)S(1)}, bf16[128,512]{1,0:T(8,128)(2,1)S(1)}, u32[]{:S(2)}, u32[]{:S(2)}) collective-permute-start(bf16[128,512]{1,0:T(8,128)(2,1)S(1)} %get-tuple-element.36), channel_id=1, source_target_pairs={{0,32},{16,48},{32,0},{48,16},{1,33},{17,49},{33,1},{49,17},{2,34}... | collective-permute-start | bytes 393224 | tf_op jit(solution)/shard_map/ppermute | solution.py:460
  191.7 11.2 %collective-permute-start.24 = (bf16[128,512]{1,0:T(8,128)(2,1)S(1)}, bf16[128,512]{1,0:T(8,128)(2,1)S(1)}, u32[]{:S(2)}, u32[]{:S(2)}) collective-permute-start(bf16[128,512]{1,0:T(8,128)(2,1)S(1)} %get-tuple-element.37), channel_id=1, source_target_pairs={{0,16},{16,32},{32,48},{48,0},{1,17},{17,33},{33,49},{49,1},{2,18}... | collective-permute-start | bytes 393224 | tf_op jit(solution)/shard_map/ppermute | solution.py:460
  (13 other events, 52.0 us)
where the time goes:
time: 207 us; the launch traced here: 205 us
  waiting for transfers between devices  72 us (35%)
  starting transfers between devices  55.4 us (27%)
  Pallas kernels  36.4 us (18%)
  blocking collectives  28 us (14%)
  local copies, waits for them, and re-layouts  7.02 us (3%)
  between operations  3.45 us (2%)
  other arithmetic  2.39 us (1%)
    ppermute x12, waiting for transfers between devices, turned(): lax.ppermute(parts[d], 'zh', [(i, (i + sign * d) % 4) for i in range(4)])  39.1 us
    all_to_all x2, blocking collectives, exchange(): return lax.all_to_all(blocks, axes, 0, 0, tiled=True)  28 us
    ppermute x12, starting transfers between devices, turned(): lax.ppermute(parts[d], 'zh', [(i, (i + sign * d) % 4) for i in range(4)])  21 us
    ppermute x4, waiting for transfers between devices, from_left(): return lax.ppermute(value, 'x', [(i, (i + 1) % 4) for i in range(4)])  20.5 us
    pallas_call x1, Pallas kernels, attend_last(): pl.pallas_call(lambda *refs: last_kernel(names, *refs), out_shape=[jax.Sh...  19.1 us
    all_to_all x2, starting transfers between devices, exchange(): return lax.all_to_all(blocks, axes, 0, 0, tiled=True)  13.3 us
    pallas_call x1, Pallas kernels, attend_first(): pl.pallas_call(lambda *refs: first_kernel(names, *refs), out_shape=jax.Sh...  11.6 us
    ppermute x3, waiting for transfers between devices, swap(): return lax.ppermute(value, axis, [(0, 1), (1, 0)])  10.1 us
  transfers between devices with their start and end apart: 30, of which 12 were waited for; matrix products, arithmetic and copies ran while one was open for 1% of the time, Pallas kernels for 7%

commit v1 on v0

--- a/solution.py
+++ b/solution.py
@@ -85,7 +85,7 @@
         ],
         compiler_params=params(),
         name="keys_payload",
-    )(keys, values, segments)
+    )(*in_hbm(keys, values, segments))
 
 
 def rows_kernel(tasks_ref, queries_ref, go_ref, pk_ref, pv_ref, *rest):
@@ -128,7 +128,7 @@
         scratch_shapes=[pltpu.SemaphoreType.DMA((6 * KVH,))],
         compiler_params=params(),
         name="rows_payload",
-    )(tasks, queries, go, prompt_keys, prompt_values)
+    )(tasks, *in_hbm(queries, go, prompt_keys, prompt_values))
     return outs[:KVH], outs[KVH : 2 * KVH], outs[2 * KVH :]
 
 
@@ -264,7 +264,7 @@
     bundles = {n: Bundle(ref) for n, ref in zip(names, refs)}
     refs = refs[len(names) :]
     att_refs, refs = refs[:KVH], refs[KVH:]
-    grads_ref, q_ref, go_ref, state_ref, acc_ref, peak_ref, sums_ref, sems = refs
+    grads_ref, q_ref, go_ref, state_ref, acc_ref, peak_ref, scores_ref, sems = refs
     zh = lax.axis_index("zh")
 
     def loaded(d):
@@ -279,38 +279,44 @@
     prompt_v = jnp.concatenate([prompt_ref[:, 2 * HD : 3 * HD], prompt_ref[:, 3 * HD :]], axis=0)
     ones = jnp.ones(prompt_v.shape, jnp.bfloat16)
     prompt_wide = jnp.concatenate([prompt_v, ones], axis=1)
-    sums_ref[...] = jnp.zeros_like(sums_ref)
+
+    blocks = range(KVH)
+    for d in blocks:
+        loaded(d).wait()
+    for d in blocks:
+        acc_ref[d, :, :HD] = state_ref[d, :, :HD]
+        acc_ref[d, :, HD:] = jnp.broadcast_to(state_ref[d, :, HD : HD + 1], (GROUP * TOK, HD))
+        peak_ref[d] = state_ref[d, :, 2 * HD - 1 :]
+        scores_ref[d] = dot_nt(q_ref[d], prompt_k)
+    for d in blocks:
+        accumulate(scores_ref[d], prompt_wide, acc_ref.at[d], peak_ref.at[d], slice(None))
 
     def per_block(d, carry):
-        loaded(d).wait()
-        q = q_ref[d]
-        acc_ref[:, :HD] = state_ref[d, :, :HD]
-        acc_ref[:, HD:] = jnp.broadcast_to(state_ref[d, :, HD : HD + 1], (GROUP * TOK, HD))
-        peak_ref[...] = state_ref[d, :, 2 * HD - 1 :]
-        accumulate(dot_nt(q, prompt_k), prompt_wide, acc_ref, peak_ref, slice(None))
-        sweep(bundles, own_ref, q, (zh - d + KVH) % KVH, acc_ref, peak_ref)
-        norm = acc_ref[:, HD:]
-        attended = (acc_ref[:, :HD] / norm).astype(jnp.bfloat16)
-        for n in range(KVH):
-
-            @pl.when(d == n)
-            def _():
-                for g in range(GROUP):
-                    att_refs[n][:, g * HD : (g + 1) * HD] = attended[g * TOK : (g + 1) * TOK]
-
+        k = (zh - d + KVH) % KVH
+        sweep(bundles, own_ref, q_ref[d], k, acc_ref.at[d], peak_ref.at[d])
+        return carry
+
+    lax.fori_loop(0, KVH, per_block, 0)
+    lows, probs_lows = [], []
+    for d in blocks:
+        norm = acc_ref[d, :, HD:]
+        attended = (acc_ref[d, :, :HD] / norm).astype(jnp.bfloat16)
+        for g in range(GROUP):
+            att_refs[d][:, g * HD : (g + 1) * HD] = attended[g * TOK : (g + 1) * TOK]
         go = go_ref[d]
         delta = jnp.sum(
             go.astype(jnp.float32) * attended.astype(jnp.float32), axis=1, keepdims=True
         )
-        log_norm = peak_ref[...] * FACTOR + jnp.log2(norm)
-        probs = jnp.exp2(dot_nt(q, prompt_k) * FACTOR - log_norm)
+        log_norm = peak_ref[d] * FACTOR + jnp.log2(norm)
+        probs = jnp.exp2(scores_ref[d] * FACTOR - log_norm)
         score_grad = probs * (dot_nt(go, prompt_v) - delta)
-        sums_ref[0:PROMPT, :] += dot_tn(score_grad.astype(jnp.bfloat16), q) * SCALE
-        sums_ref[PROMPT:, :] += dot_tn(probs.astype(jnp.bfloat16), go)
-        return carry
-
-    lax.fori_loop(0, KVH, per_block, 0)
-    grads_ref[...] = sums_ref[...].astype(jnp.bfloat16)
+        lows.append(score_grad.astype(jnp.bfloat16))
+        probs_lows.append(probs.astype(jnp.bfloat16))
+    everything = (KVH * GROUP * TOK, HD)
+    key_part = dot_tn(jnp.concatenate(lows, axis=0), q_ref[...].reshape(everything)) * SCALE
+    value_part = dot_tn(jnp.concatenate(probs_lows, axis=0), go_ref[...].reshape(everything))
+    grads_ref[0:PROMPT, :] = key_part.astype(jnp.bfloat16)
+    grads_ref[PROMPT:, :] = value_part.astype(jnp.bfloat16)
 
 
 def attend_last(names, q, go, state, own, prompt, arrays):
@@ -326,9 +332,9 @@
             pltpu.VMEM((KVH, GROUP * TOK, HD), jnp.bfloat16),
             pltpu.VMEM((KVH, GROUP * TOK, HD), jnp.bfloat16),
             pltpu.VMEM(STATE, jnp.float32),
-            pltpu.VMEM((GROUP * TOK, 2 * HD), jnp.float32),
-            pltpu.VMEM((GROUP * TOK, 1), jnp.float32),
-            pltpu.VMEM((2 * PROMPT, HD), jnp.float32),
+            pltpu.VMEM((KVH, GROUP * TOK, 2 * HD), jnp.float32),
+            pltpu.VMEM((KVH, GROUP * TOK, 1), jnp.float32),
+            pltpu.VMEM((KVH, GROUP * TOK, HD), jnp.float32),
             pltpu.SemaphoreType.DMA((KVH,)),
         ],
         compiler_params=params(),
@@ -466,18 +472,38 @@
     return lax.all_to_all(blocks, axes, 0, 0, tiled=True)
 
 
-def choose(index, own, others):
-    chosen = own
-    for position, other in others:
-        chosen = jnp.where(index == position, other, chosen)
-    return chosen
+def choose_kernel(stage, tasks_ref, *refs):
+    parts, out_ref = refs[:KVH], refs[KVH]
+    owner = tasks_ref[lax.axis_index("dp")] // 2
+    if stage == "zh":
+        wanted = (lax.axis_index("zh") + KVH - owner // 16) % KVH
+    elif stage == "zl_y":
+        zl, y = lax.axis_index("zl"), lax.axis_index("y")
+        wanted = ((owner // 8 + zl) % 2) * 2 + (owner + y) % 2
+    else:
+        wanted = (lax.axis_index("x") + 4 - (owner // 2) % 4) % 4
+    for n in range(KVH):
+
+        @pl.when(wanted == n)
+        def _():
+            out_ref[...] = parts[n][...]
+
+
+def choose(stage, tasks, parts):
+    return pl.pallas_call(
+        lambda *refs: choose_kernel(stage, *refs),
+        out_shape=jax.ShapeDtypeStruct(parts[0].shape, parts[0].dtype),
+        in_specs=[SMEM] + [VMEM] * KVH,
+        out_specs=VMEM,
+        compiler_params=params(4),
+    )(tasks, *parts)
+
+
+def in_hbm(*arrays):
+    return [pltpu.with_memory_space_constraint(array, pltpu.HBM) for array in arrays]
 
 
 def step(queries, keys, values, segments, task_ids, prompt_keys, prompt_values, grad_out):
-    dp, zh, zl, x, y = (lax.axis_index(name) for name in ALL)
-    owner = task_ids[dp] // 2
-    own_zh, own_zl, own_x, own_y = owner // 16, (owner // 8) % 2, (owner // 2) % 4, owner % 2
-
     payload = keys_payload(keys, values, segments)
     own = exchange(payload, ("zh", "zl"))
     q, go, prompts = rows_payload(
@@ -495,16 +521,15 @@
     beside_right = from_right(beside)
     go = turned(go, 1)
 
-    prompt = choose((zh - own_zh) % KVH, prompts[0], list(enumerate(prompts))[1:])
-    flip_zl, flip_y = (own_zl != zl).astype(jnp.int32), (own_y != y).astype(jnp.int32)
+    prompt = choose("zh", task_ids, prompts)
     both = lax.ppermute(prompt, ("zl", "y"), [(i, 3 - i) for i in range(4)])
     flipped = swap(prompt, "zl")
     beyond = swap(prompt, "y")
-    prompt = choose(flip_zl * 2 + flip_y, prompt, [(2, flipped), (1, beyond), (3, both)])
+    prompt = choose("zl_y", task_ids, (prompt, beyond, flipped, both))
     far = lax.ppermute(prompt, "x", [(i, (i + 2) % 4) for i in range(4)])
-    sides = [((x + 3) % 4, from_left(prompt))]
-    sides.append(((x + 1) % 4, from_right(prompt)))
-    prompt = choose(own_x, prompt, sides + [((x + 2) % 4, far)])
+    prompt_left = from_left(prompt)
+    prompt_right = from_right(prompt)
+    prompt = choose("x", task_ids, (prompt, prompt_left, far, prompt_right))
 
     state = attend_first((0, 1, 2, 3), q, (own, beside, left, right))
     attended, grads = attend_last(

time: 207 us -> 200 us (0.966)
  blocking collectives: 28 us -> 48.8 us
  starting transfers between devices: 55.4 us -> 41.9 us
  local copies, waits for them, and re-layouts: 7.02 us -> 0.66 us
  between operations: 3.45 us -> 0.79 us
  other arithmetic: 2.39 us -> 0 us
  Pallas kernels: 36.4 us -> 34.2 us
    all_to_all x2 -> x3, blocking collectives: 28 us -> 48.8 us  [exchange(): return lax.all_to_all(blocks, axes, 0, 0, tiled=True)]
    ppermute x4, waiting for transfers between devices: 20.5 us -> 0.01 us  [from_left(): return lax.ppermute(value, 'x', [(i, (i + 1) % 4) for i in range(4)])]
    ppermute x1, waiting for transfers between devices: 0.01 us -> 12.9 us  [step(): far = lax.ppermute(prompt, 'x', [(i, (i + 2) % 4) for i in range(4)])]
    all_to_all x2 -> x1, starting transfers between devices: 13.3 us -> 4.86 us  [exchange(): return lax.all_to_all(blocks, axes, 0, 0, tiled=True)]
    ppermute x3, waiting for transfers between devices: 10.1 us -> 3.38 us  [swap(): return lax.ppermute(value, axis, [(0, 1), (1, 0)])]
    unnamed x30 -> x4, local copies, waits for them, and re-layouts: 6.41 us -> 0.66 us
    ppermute x1, waiting for transfers between devices: 0.01 us -> 5.23 us  [step(): both = lax.ppermute(prompt, ('zl', 'y'), [(i, 3 - i) for i in range(4)])]
    pallas_call x1, Pallas kernels: 19.1 us -> 13.9 us  [attend_last(): pl.pallas_call(lambda *refs: last_kernel(names, *refs), out_shape=[jax.Sh...]
  transfers between devices with their start and end apart: 30 -> 29, of which waited for: 12 -> 15; matrix products, arithmetic and copies ran while one was open for 1% -> 0% of each run, Pallas kernels for 7% -> 8%
where the time goes in v1:
time: 200 us; the launch traced here: 198 us
  waiting for transfers between devices  71.2 us (36%)
  blocking collectives  48.8 us (24%)
  starting transfers between devices  41.9 us (21%)
  Pallas kernels  34.2 us (17%)
    all_to_all x3, blocking collectives, exchange(): return lax.all_to_all(blocks, axes, 0, 0, tiled=True)  48.8 us
    ppermute x12, waiting for transfers between devices, turned(): lax.ppermute(parts[d], 'zh', [(i, (i + sign * d) % 4) for i in range(4)])  40.5 us
    ppermute x12, starting transfers between devices, turned(): lax.ppermute(parts[d], 'zh', [(i, (i + sign * d) % 4) for i in range(4)])  19.2 us
    pallas_call x1, Pallas kernels, attend_last(): pl.pallas_call(lambda *refs: last_kernel(names, *refs), out_shape=[jax.Sh...  13.9 us
    ppermute x1, waiting for transfers between devices, step(): far = lax.ppermute(prompt, 'x', [(i, (i + 2) % 4) for i in range(4)])  12.9 us
    pallas_call x1, Pallas kernels, attend_first(): pl.pallas_call(lambda *refs: first_kernel(names, *refs), out_shape=jax.Sh...  11.6 us
    ppermute x1, waiting for transfers between devices, step(): both = lax.ppermute(prompt, ('zl', 'y'), [(i, 3 - i) for i in range(4)])  5.23 us
    ppermute x3, waiting for transfers between devices, step(): parts.append(lax.ppermute(mine, 'dp', [(i, i ^ d) for i in range(4)]))  4.86 us
  transfers between devices with their start and end apart: 29, of which 15 were waited for; matrix products, arithmetic and copies ran while one was open for 0% of the time, Pallas kernels for 8%

profile of v1, /device:TPU:2, one launch (start us, length us, event | category | flops | bytes accessed | tf_op | source)
XLA Modules:
  0.0 197.5 jit_solution(8381084270341826661)
XLA Ops:
  1.8 26.5 %all_to_all.20.refs_4_.refs_9_ = bf16[8,272,128]{2,1,0:T(8,128)(2,1)S(1)} all-to-all(bf16[8,272,128]{2,1,0:T(8,128)(2,1)S(1)} %keys_payload.1), channel_id=1, replica_groups=mesh['dp'=4,'zh'=4,'zl'=2,'x'=4,'y'=2] {'zh','zl'}, dimensions={0} | all-to-all | bytes 1114112 | tf_op jit(solution)/shard_map/all_to_all | solution.py:472
  28.3 1.6 collective-permute-start.6
  29.8 1.5 collective-permute-start.7
  32.5 2.2 %rows_payload.1 = (bf16[128,512]{1,0:T(8,128)(2,1)S(1)}, bf16[128,512]{1,0:T(8,128)(2,1)S(1)}, bf16[128,512]{1,0:T(8,128)(2,1)S(1)}, bf16[128,512]{1,0:T(8,128)(...) custom-call(s32[4]{0:T(128)S(1)} %copy-done, ...), custom_call_target="tpu_custom_call" | custom-call | tf_op jit(solution)/shard_map/rows_payload/pallas_call | solution.py:122
  35.4 3.5 %collective-permute-start.11 = (bf16[64,512]{1,0:T(8,128)(2,1)S(1)}, bf16[64,512]{1,0:T(8,128)(2,1)S(1)}, u32[]{:S(2)}, u32[]{:S(2)}) collective-permute-start(bf16[64,512]{1,0:T(8,128)(2,1)S(1)} %get-tuple-element.33), channel_id=1, source_target_pairs={{0,48},{16,0},{32,16},{48,32},{1,49},{17,1},{33,17},{49,33},{2,50}... | collective-permute-start | bytes 196616 | tf_op jit(solution)/shard_map/ppermute | solution.py:466
  38.9 4.3 %collective-permute-done.10.refs_3_ = bf16[64,512]{1,0:T(8,128)(2,1)S(1)} collective-permute-done((bf16[64,512]{1,0:T(8,128)(2,1)S(1)}, bf16[64,512]{1,0:T(8,128)(2,1)S(1)}, u32[]{:S(2)}, u32[]{:S(2)}) %collective-permute-start.10) | collective-permute-done | bytes 65568 | tf_op jit(solution)/shard_map/ppermute | solution.py:466
  43.7 6.4 %collective-permute-done.9.refs_2_ = bf16[64,512]{1,0:T(8,128)(2,1)S(1)} collective-permute-done((bf16[64,512]{1,0:T(8,128)(2,1)S(1)}, bf16[64,512]{1,0:T(8,128)(2,1)S(1)}, u32[]{:S(2)}, u32[]{:S(2)}) %collective-permute-start.9) | collective-permute-done | bytes 65568 | tf_op jit(solution)/shard_map/ppermute | solution.py:466
  52.0 3.1 %collective-permute-done.12.refs_2_ = bf16[64,512]{1,0:T(8,128)(2,1)S(1)} collective-permute-done((bf16[64,512]{1,0:T(8,128)(2,1)S(1)}, bf16[64,512]{1,0:T(8,128)(2,1)S(1)}, u32[]{:S(2)}, u32[]{:S(2)}) %collective-permute-start.12) | collective-permute-done | bytes 65568 | tf_op jit(solution)/shard_map/ppermute | solution.py:446
  56.0 5.2 %collective-permute-done.14.refs_4_ = bf16[64,512]{1,0:T(8,128)(2,1)S(1)} collective-permute-done((bf16[64,512]{1,0:T(8,128)(2,1)S(1)}, bf16[64,512]{1,0:T(8,128)(2,1)S(1)}, u32[]{:S(2)}, u32[]{:S(2)}) %collective-permute-start.14) | collective-permute-done | bytes 65568 | tf_op jit(solution)/shard_map/ppermute | solution.py:525
  61.2 1.2 collective-permute-start.1
  63.7 9.6 %collective-permute-done.1.refs_2_ = bf16[128,512]{1,0:T(8,128)(2,1)S(1)} collective-permute-done((bf16[128,512]{1,0:T(8,128)(2,1)S(1)}, bf16[128,512]{1,0:T(8,128)(2,1)S(1)}, u32[]{:S(2)}, u32[]{:S(2)}) %collective-permute-start.1) | collective-permute-done | bytes 131104 | tf_op jit(solution)/shard_map/ppermute | solution.py:466
  73.9 1.6 collective-permute-start.15
  75.5 1.2 collective-permute-start.19
  76.7 3.7 %collective-permute-done.3.refs_5_ = bf16[128,512]{1,0:T(8,128)(2,1)S(1)} collective-permute-done((bf16[128,512]{1,0:T(8,128)(2,1)S(1)}, bf16[128,512]{1,0:T(8,128)(2,1)S(1)}, u32[]{:S(2)}, u32[]{:S(2)}) %collective-permute-start.3) | collective-permute-done | bytes 131104 | tf_op jit(solution)/shard_map/ppermute | solution.py:466
  80.4 1.7 collective-permute-start.20
  82.9 2.9 %collective-permute-start.16 = (bf16[64,512]{1,0:T(8,128)(2,1)S(1)}, bf16[64,512]{1,0:T(8,128)(2,1)S(1)}, u32[]{:S(2)}, u32[]{:S(2)}) collective-permute-start(bf16[64,512]{1,0:T(8,128)(2,1)S(1)} %shard_map.104.refs_1_), channel_id=1, source_target_pairs={{0,4},{2,6},{4,0},{6,2},{1,5},{3,7},{5,1},{7,3},{8,12},{10,14},{12... | collective-permute-start | bytes 196616 | tf_op jit(solution)/shard_map/ppermute | solution.py:529
  85.8 12.9 %collective-permute-done.16.refs_3_ = bf16[64,512]{1,0:T(8,128)(2,1)S(1)} collective-permute-done((bf16[64,512]{1,0:T(8,128)(2,1)S(1)}, bf16[64,512]{1,0:T(8,128)(2,1)S(1)}, u32[]{:S(2)}, u32[]{:S(2)}) %collective-permute-start.16) | collective-permute-done | bytes 65568 | tf_op jit(solution)/shard_map/ppermute | solution.py:529
  98.7 4.3 %collective-permute-done.17.refs_4_ = bf16[64,512]{1,0:T(8,128)(2,1)S(1)} collective-permute-done((bf16[64,512]{1,0:T(8,128)(2,1)S(1)}, bf16[64,512]{1,0:T(8,128)(2,1)S(1)}, u32[]{:S(2)}, u32[]{:S(2)}) %collective-permute-start.17) | collective-permute-done | bytes 65568 | tf_op jit(solution)/shard_map/ppermute | solution.py:454
  103.0 3.7 %collective-permute-start.4 = (bf16[128,512]{1,0:T(8,128)(2,1)S(1)}, bf16[128,512]{1,0:T(8,128)(2,1)S(1)}, u32[]{:S(2)}, u32[]{:S(2)}) collective-permute-start(bf16[128,512]{1,0:T(8,128)(2,1)S(1)} %get-tuple-element.28), channel_id=1, source_target_pairs={{0,32},{16,48},{32,0},{48,16},{1,33},{17,49},{33,1},{49,17},{2,34}... | collective-permute-start | bytes 393224 | tf_op jit(solution)/shard_map/ppermute | solution.py:466
  107.2 4.7 %collective-permute-done.4.refs_6_ = bf16[128,512]{1,0:T(8,128)(2,1)S(1)} collective-permute-done((bf16[128,512]{1,0:T(8,128)(2,1)S(1)}, bf16[128,512]{1,0:T(8,128)(2,1)S(1)}, u32[]{:S(2)}, u32[]{:S(2)}) %collective-permute-start.4) | collective-permute-done | bytes 131104 | tf_op jit(solution)/shard_map/ppermute | solution.py:466
  111.9 5.0 %collective-permute-start.5 = (bf16[128,512]{1,0:T(8,128)(2,1)S(1)}, bf16[128,512]{1,0:T(8,128)(2,1)S(1)}, u32[]{:S(2)}, u32[]{:S(2)}) collective-permute-start(bf16[128,512]{1,0:T(8,128)(2,1)S(1)} %get-tuple-element.29), channel_id=1, source_target_pairs={{0,48},{16,0},{32,16},{48,32},{1,49},{17,1},{33,17},{49,33},{2,50}... | collective-permute-start | bytes 393224 | tf_op jit(solution)/shard_map/ppermute | solution.py:466
  116.9 11.6 %attend_first.1.refs_8_ = f32[4,512,256]{2,1,0:T(8,128)S(1)} custom-call(bf16[128,512]{1,0:T(8,128)(2,1)S(1)} %get-tuple-element.22.refs_0_, bf16[128,512]{1,0:T(8,128)(2,1)S(1)} %collective-permute-done.refs_1_, bf16[128,512]{1,0:T(8,128)(2,1)S(1)} %collective-permute-done.1.refs_2_, bf16[128,512]{1,0:T(8,128)(2,1)S(1)} %collective-permute-done.2.refs_3_, ...), custom_call_target="tpu_custom_call" | custom-call | flops 2684354560 | bytes 4194304 | tf_op jit(solution)/shard_map/attend_first/pallas_call | solution.py:243
  128.6 13.9 %attend_last.1 = (bf16[128,512]{1,0:T(8,128)(2,1)S(1)}, bf16[128,512]{1,0:T(8,128)(2,1)S(1)}, bf16[128,512]{1,0:T(8,128)(2,1)S(1)}, bf16[128,512]{1,0:T(8,128)(2,1)S(1)}, bf16[256,128]{1,0:T(8,128)(2,1)S(1)}) custom-call(bf16[128,512]{1,0:T(8,128)(2,1)S(1)} %get-tuple-element.22.refs_0_, bf16[128,512]{1,0:T(8,128)(2,1)S(1)} %collective-permute-done.refs_1_, ...), custom_call_target="tpu_custom_call" | custom-call | flops 3355443200 | bytes 4194304 | tf_op jit(solution)/shard_map/attend_last/pallas_call | solution.py:323
  142.5 10.7 %all_to_all.21.pieces_ref = bf16[8,32,128]{2,1,0:T(8,128)(2,1)S(1)} all-to-all(bf16[8,32,128]{2,1,0:T(8,128)(2,1)S(1)} %bitcast.1), channel_id=1, replica_groups=mesh['dp'=4,'zh'=4,'zl'=2,'x'=4,'y'=2] {'x','y'}, dimensions={0} | all-to-all | bytes 131072 | tf_op jit(solution)/shard_map/all_to_all | solution.py:472
  153.2 11.7 %all_to_all.22.sent_ref = bf16[8,32,128]{2,1,0:T(8,128)(2,1)S(1)} all-to-all(bf16[8,32,128]{2,1,0:T(8,128)(2,1)S(1)} %summed.1), channel_id=1, replica_groups=mesh['dp'=4,'zh'=4,'zl'=2,'x'=4,'y'=2] {'zh','zl'}, dimensions={0} | all-to-all | bytes 131072 | tf_op jit(solution)/shard_map/all_to_all | solution.py:472
  165.0 4.1 %collective-permute-start.26 = (bf16[4,32,128]{2,1,0:T(8,128)(2,1)S(1)}, bf16[4,32,128]{2,1,0:T(8,128)(2,1)S(1)}, u32[]{:S(2)}, u32[]{:S(2)}) collective-permute-start(bf16[4,32,128]{2,1,0:T(8,128)(2,1)S(1)} %pairs_summed.1.refs_0_), channel_id=1, source_target_pairs={{0,128},{64,192},{128,0},{192,64},{1,129},{65,193},{129,1},{193,65... | collective-permute-start | bytes 98312 | tf_op jit(solution)/shard_map/ppermute | solution.py:551
  169.1 1.9 collective-permute-done.26.refs_2_
  171.0 2.9 %collective-permute-done.27.refs_3_ = bf16[4,32,128]{2,1,0:T(8,128)(2,1)S(1)} collective-permute-done((bf16[4,32,128]{2,1,0:T(8,128)(2,1)S(1)}, bf16[4,32,128]{2,1,0:T(8,128)(2,1)S(1)}, u32[]{:S(2)}, u32[]{:S(2)}) %collective-permute-start.27) | collective-permute-done | bytes 32800 | tf_op jit(solution)/shard_map/ppermute | solution.py:551
  174.0 1.7 route.1
  175.6 4.9 %all-to-all-start.3 = ((bf16[8,2,4,32,128]{4,3,2,1,0:T(8,128)(2,1)}), bf16[8,2,4,32,128]{4,3,2,1,0:T(8,128)(2,1)S(1)}, u32[]{:S(2)}, u32[]{:S(2)}) async-start(bf16[8,2,4,32,128]{4,3,2,1,0:T(8,128)(2,1)} %route.1), calls=%async_computation.3 | async-start | bytes 1048576 | tf_op jit(solution)/shard_map/all_to_all | solution.py:472
  180.9 3.7 %collective-permute-start.23 = (bf16[128,512]{1,0:T(8,128)(2,1)S(1)}, bf16[128,512]{1,0:T(8,128)(2,1)S(1)}, u32[]{:S(2)}, u32[]{:S(2)}) collective-permute-start(bf16[128,512]{1,0:T(8,128)(2,1)S(1)} %get-tuple-element.36), channel_id=1, source_target_pairs={{0,32},{16,48},{32,0},{48,16},{1,33},{17,49},{33,1},{49,17},{2,34}... | collective-permute-start | bytes 393224 | tf_op jit(solution)/shard_map/ppermute | solution.py:466
  184.6 10.3 %collective-permute-done.22.refs_1_ = bf16[128,512]{1,0:T(8,128)(2,1)S(1)} collective-permute-done((bf16[128,512]{1,0:T(8,128)(2,1)S(1)}, bf16[128,512]{1,0:T(8,128)(2,1)S(1)}, u32[]{:S(2)}, u32[]{:S(2)}) %collective-permute-start.22) | collective-permute-done | bytes 131104 | tf_op jit(solution)/shard_map/ppermute | solution.py:466
  (45 shorter events, 12.8 us)
Async XLA Ops:
  28.3 47.2 %collective-permute-start.6 = (bf16[8,272,128]{2,1,0:T(8,128)(2,1)S(1)}, bf16[8,272,128]{2,1,0:T(8,128)(2,1)S(1)}, u32[]{:S(2)}, u32[]{:S(2)}) collective-permute-start(bf16[8,272,128]{2,1,0:T(8,128)(2,1)S(1)} %all_to_all.20.refs_4_.refs_9_), channel_id=1, source_target_pairs={{0,1},{1,0},{2,3},{3,2},{4,5},{5,4},{6,7},{7,6},{8,9},{9,8},{10,11... | collective-permute-start | bytes 1671176 | tf_op jit(solution)/shard_map/ppermute | solution.py:446
  29.8 52.3 %collective-permute-start.7 = (bf16[8,272,128]{2,1,0:T(8,128)(2,1)S(1)}, bf16[8,272,128]{2,1,0:T(8,128)(2,1)S(1)}, u32[]{:S(2)}, u32[]{:S(2)}) collective-permute-start(bf16[8,272,128]{2,1,0:T(8,128)(2,1)S(1)} %all_to_all.20.refs_4_.refs_9_), channel_id=1, source_target_pairs={{0,2},{2,4},{4,6},{6,0},{1,3},{3,5},{5,7},{7,1},{8,10},{10,12},{12... | collective-permute-start | bytes 1671176 | tf_op jit(solution)/shard_map/ppermute | solution.py:450
  31.3 51.1 %collective-permute-start.8 = (bf16[8,272,128]{2,1,0:T(8,128)(2,1)S(1)}, bf16[8,272,128]{2,1,0:T(8,128)(2,1)S(1)}, u32[]{:S(2)}, u32[]{:S(2)}) collective-permute-start(bf16[8,272,128]{2,1,0:T(8,128)(2,1)S(1)} %all_to_all.20.refs_4_.refs_9_), channel_id=1, source_target_pairs={{0,6},{2,0},{4,2},{6,4},{1,7},{3,1},{5,3},{7,5},{8,14},{10,8},{12,... | collective-permute-start | bytes 1671176 | tf_op jit(solution)/shard_map/ppermute | solution.py:454
  31.9 0.7 copy-start
  34.7 8.4 %collective-permute-start.10 = (bf16[64,512]{1,0:T(8,128)(2,1)S(1)}, bf16[64,512]{1,0:T(8,128)(2,1)S(1)}, u32[]{:S(2)}, u32[]{:S(2)}) collective-permute-start(bf16[64,512]{1,0:T(8,128)(2,1)S(1)} %get-tuple-element.32), channel_id=1, source_target_pairs={{0,32},{16,48},{32,0},{48,16},{1,33},{17,49},{33,1},{49,17},{2,34}... | collective-permute-start | bytes 196616 | tf_op jit(solution)/shard_map/ppermute | solution.py:466
  35.4 8.3 %collective-permute-start.11 = (bf16[64,512]{1,0:T(8,128)(2,1)S(1)}, bf16[64,512]{1,0:T(8,128)(2,1)S(1)}, u32[]{:S(2)}, u32[]{:S(2)}) collective-permute-start(bf16[64,512]{1,0:T(8,128)(2,1)S(1)} %get-tuple-element.33), channel_id=1, source_target_pairs={{0,48},{16,0},{32,16},{48,32},{1,49},{17,1},{33,17},{49,33},{2,50}... | collective-permute-start | bytes 196616 | tf_op jit(solution)/shard_map/ppermute | solution.py:466
  43.2 7.0 %collective-permute-start.9 = (bf16[64,512]{1,0:T(8,128)(2,1)S(1)}, bf16[64,512]{1,0:T(8,128)(2,1)S(1)}, u32[]{:S(2)}, u32[]{:S(2)}) collective-permute-start(bf16[64,512]{1,0:T(8,128)(2,1)S(1)} %get-tuple-element.31), channel_id=1, source_target_pairs={{0,16},{16,32},{32,48},{48,0},{1,17},{17,33},{33,49},{49,1},{2,18}... | collective-permute-start | bytes 196616 | tf_op jit(solution)/shard_map/ppermute | solution.py:466
  50.7 4.4 %collective-permute-start.12 = (bf16[64,512]{1,0:T(8,128)(2,1)S(1)}, bf16[64,512]{1,0:T(8,128)(2,1)S(1)}, u32[]{:S(2)}, u32[]{:S(2)}) collective-permute-start(bf16[64,512]{1,0:T(8,128)(2,1)S(1)} %shard_map.103.refs_1_), channel_id=1, source_target_pairs={{0,1},{1,0},{2,3},{3,2},{4,5},{5,4},{6,7},{7,6},{8,9},{9,8},{10,11... | collective-permute-start | bytes 196616 | tf_op jit(solution)/shard_map/ppermute | solution.py:446
  51.7 4.3 %collective-permute-start.13 = (bf16[64,512]{1,0:T(8,128)(2,1)S(1)}, bf16[64,512]{1,0:T(8,128)(2,1)S(1)}, u32[]{:S(2)}, u32[]{:S(2)}) collective-permute-start(bf16[64,512]{1,0:T(8,128)(2,1)S(1)} %shard_map.103.refs_1_), channel_id=1, source_target_pairs={{0,8},{8,0},{1,9},{9,1},{2,10},{10,2},{3,11},{11,3},{4,12},{12,4},... | collective-permute-start | bytes 196616 | tf_op jit(solution)/shard_map/ppermute | solution.py:446
  55.1 6.1 %collective-permute-start.14 = (bf16[64,512]{1,0:T(8,128)(2,1)S(1)}, bf16[64,512]{1,0:T(8,128)(2,1)S(1)}, u32[]{:S(2)}, u32[]{:S(2)}) collective-permute-start(bf16[64,512]{1,0:T(8,128)(2,1)S(1)} %shard_map.103.refs_1_), channel_id=1, source_target_pairs={{0,9},{1,8},{8,1},{9,0},{2,11},{3,10},{10,3},{11,2},{4,13},{5,12},... | collective-permute-start | bytes 196616 | tf_op jit(solution)/shard_map/ppermute | solution.py:525
  56.0 7.2 %collective-permute-start = (bf16[128,512]{1,0:T(8,128)(2,1)S(1)}, bf16[128,512]{1,0:T(8,128)(2,1)S(1)}, u32[]{:S(2)}, u32[]{:S(2)}) collective-permute-start(bf16[128,512]{1,0:T(8,128)(2,1)S(1)} %get-tuple-element.23), channel_id=1, source_target_pairs={{0,16},{16,32},{32,48},{48,0},{1,17},{17,33},{33,49},{49,1},{2,18}... | collective-permute-start | bytes 393224 | tf_op jit(solution)/shard_map/ppermute | solution.py:466
  61.2 12.1 %collective-permute-start.1 = (bf16[128,512]{1,0:T(8,128)(2,1)S(1)}, bf16[128,512]{1,0:T(8,128)(2,1)S(1)}, u32[]{:S(2)}, u32[]{:S(2)}) collective-permute-start(bf16[128,512]{1,0:T(8,128)(2,1)S(1)} %get-tuple-element.24), channel_id=1, source_target_pairs={{0,32},{16,48},{32,0},{48,16},{1,33},{17,49},{33,1},{49,17},{2,34}... | collective-permute-start | bytes 393224 | tf_op jit(solution)/shard_map/ppermute | solution.py:466
  63.1 10.8 %collective-permute-start.2 = (bf16[128,512]{1,0:T(8,128)(2,1)S(1)}, bf16[128,512]{1,0:T(8,128)(2,1)S(1)}, u32[]{:S(2)}, u32[]{:S(2)}) collective-permute-start(bf16[128,512]{1,0:T(8,128)(2,1)S(1)} %get-tuple-element.25), channel_id=1, source_target_pairs={{0,48},{16,0},{32,16},{48,32},{1,49},{17,1},{33,17},{49,33},{2,50}... | collective-permute-start | bytes 393224 | tf_op jit(solution)/shard_map/ppermute | solution.py:466
  73.3 7.1 %collective-permute-start.3 = (bf16[128,512]{1,0:T(8,128)(2,1)S(1)}, bf16[128,512]{1,0:T(8,128)(2,1)S(1)}, u32[]{:S(2)}, u32[]{:S(2)}) collective-permute-start(bf16[128,512]{1,0:T(8,128)(2,1)S(1)} %get-tuple-element.27), channel_id=1, source_target_pairs={{0,16},{16,32},{32,48},{48,0},{1,17},{17,33},{33,49},{49,1},{2,18}... | collective-permute-start | bytes 393224 | tf_op jit(solution)/shard_map/ppermute | solution.py:466
  73.9 9.0 %collective-permute-start.15 = (bf16[64,512]{1,0:T(8,128)(2,1)S(1)}, bf16[64,512]{1,0:T(8,128)(2,1)S(1)}, u32[]{:S(2)}, u32[]{:S(2)}) collective-permute-start(bf16[64,512]{1,0:T(8,128)(2,1)S(1)} %shard_map.104.refs_1_), channel_id=1, source_target_pairs={{0,2},{2,4},{4,6},{6,0},{1,3},{3,5},{5,7},{7,1},{8,10},{10,12},{12... | collective-permute-start | bytes 196616 | tf_op jit(solution)/shard_map/ppermute | solution.py:450
  75.5 53.0 %collective-permute-start.19 = (bf16[8,272,128]{2,1,0:T(8,128)(2,1)S(1)}, bf16[8,272,128]{2,1,0:T(8,128)(2,1)S(1)}, u32[]{:S(2)}, u32[]{:S(2)}) collective-permute-start(bf16[8,272,128]{2,1,0:T(8,128)(2,1)S(1)} %collective-permute-done.6.refs_5_), channel_id=1, source_target_pairs={{0,2},{2,4},{4,6},{6,0},{1,3},{3,5},{5,7},{7,1},{8,10},{10,12},{12... | collective-permute-start | bytes 1671176 | tf_op jit(solution)/shard_map/ppermute | solution.py:450
  80.4 48.2 %collective-permute-start.20 = (bf16[8,272,128]{2,1,0:T(8,128)(2,1)S(1)}, bf16[8,272,128]{2,1,0:T(8,128)(2,1)S(1)}, u32[]{:S(2)}, u32[]{:S(2)}) collective-permute-start(bf16[8,272,128]{2,1,0:T(8,128)(2,1)S(1)} %collective-permute-done.6.refs_5_), channel_id=1, source_target_pairs={{0,6},{2,0},{4,2},{6,4},{1,7},{3,1},{5,3},{7,5},{8,14},{10,8},{12,... | collective-permute-start | bytes 1671176 | tf_op jit(solution)/shard_map/ppermute | solution.py:454
  82.1 46.4 %collective-permute-start.18 = (bf16[8,272,128]{2,1,0:T(8,128)(2,1)S(1)}, bf16[8,272,128]{2,1,0:T(8,128)(2,1)S(1)}, u32[]{:S(2)}, u32[]{:S(2)}) collective-permute-start(bf16[8,272,128]{2,1,0:T(8,128)(2,1)S(1)} %collective-permute-done.7.refs_6_), channel_id=1, source_target_pairs={{0,2},{2,4},{4,6},{6,0},{1,3},{3,5},{5,7},{7,1},{8,10},{10,12},{12... | collective-permute-start | bytes 1671176 | tf_op jit(solution)/shard_map/ppermute | solution.py:450
  82.4 46.1 %collective-permute-start.21 = (bf16[8,272,128]{2,1,0:T(8,128)(2,1)S(1)}, bf16[8,272,128]{2,1,0:T(8,128)(2,1)S(1)}, u32[]{:S(2)}, u32[]{:S(2)}) collective-permute-start(bf16[8,272,128]{2,1,0:T(8,128)(2,1)S(1)} %collective-permute-done.8.refs_7_), channel_id=1, source_target_pairs={{0,7},{1,6},{2,1},{3,0},{4,3},{5,2},{6,5},{7,4},{8,15},{9,14},{10,... | collective-permute-start | bytes 1671176 | tf_op jit(solution)/shard_map/ppermute | solution.py:459
  82.9 15.8 %collective-permute-start.16 = (bf16[64,512]{1,0:T(8,128)(2,1)S(1)}, bf16[64,512]{1,0:T(8,128)(2,1)S(1)}, u32[]{:S(2)}, u32[]{:S(2)}) collective-permute-start(bf16[64,512]{1,0:T(8,128)(2,1)S(1)} %shard_map.104.refs_1_), channel_id=1, source_target_pairs={{0,4},{2,6},{4,0},{6,2},{1,5},{3,7},{5,1},{7,3},{8,12},{10,14},{12... | collective-permute-start | bytes 196616 | tf_op jit(solution)/shard_map/ppermute | solution.py:529
  98.7 4.3 %collective-permute-start.17 = (bf16[64,512]{1,0:T(8,128)(2,1)S(1)}, bf16[64,512]{1,0:T(8,128)(2,1)S(1)}, u32[]{:S(2)}, u32[]{:S(2)}) collective-permute-start(bf16[64,512]{1,0:T(8,128)(2,1)S(1)} %shard_map.104.refs_1_), channel_id=1, source_target_pairs={{0,6},{2,0},{4,2},{6,4},{1,7},{3,1},{5,3},{7,5},{8,14},{10,8},{12,... | collective-permute-start | bytes 196616 | tf_op jit(solution)/shard_map/ppermute | solution.py:454
  103.0 8.9 %collective-permute-start.4 = (bf16[128,512]{1,0:T(8,128)(2,1)S(1)}, bf16[128,512]{1,0:T(8,128)(2,1)S(1)}, u32[]{:S(2)}, u32[]{:S(2)}) collective-permute-start(bf16[128,512]{1,0:T(8,128)(2,1)S(1)} %get-tuple-element.28), channel_id=1, source_target_pairs={{0,32},{16,48},{32,0},{48,16},{1,33},{17,49},{33,1},{49,17},{2,34}... | collective-permute-start | bytes 393224 | tf_op jit(solution)/shard_map/ppermute | solution.py:466
  111.9 16.6 %collective-permute-start.5 = (bf16[128,512]{1,0:T(8,128)(2,1)S(1)}, bf16[128,512]{1,0:T(8,128)(2,1)S(1)}, u32[]{:S(2)}, u32[]{:S(2)}) collective-permute-start(bf16[128,512]{1,0:T(8,128)(2,1)S(1)} %get-tuple-element.29), channel_id=1, source_target_pairs={{0,48},{16,0},{32,16},{48,32},{1,49},{17,1},{33,17},{49,33},{2,50}... | collective-permute-start | bytes 393224 | tf_op jit(solution)/shard_map/ppermute | solution.py:466
  128.6 45.4 %copy-start.1 = (s32[4]{0:T(128)S(1)}, s32[4]{0:T(128)}, u32[]{:S(2)}) copy-start(s32[4]{0:T(128)} %tasks_ref.3) | copy-start | bytes 52
  164.9 4.2 %collective-permute-start.25 = (bf16[4,32,128]{2,1,0:T(8,128)(2,1)S(1)}, bf16[4,32,128]{2,1,0:T(8,128)(2,1)S(1)}, u32[]{:S(2)}, u32[]{:S(2)}) collective-permute-start(bf16[4,32,128]{2,1,0:T(8,128)(2,1)S(1)} %pairs_summed.1.refs_0_), channel_id=1, source_target_pairs={{0,64},{64,0},{128,192},{192,128},{1,65},{65,1},{129,193},{193,129... | collective-permute-start | bytes 98312 | tf_op jit(solution)/shard_map/ppermute | solution.py:551
  165.0 6.0 %collective-permute-start.26 = (bf16[4,32,128]{2,1,0:T(8,128)(2,1)S(1)}, bf16[4,32,128]{2,1,0:T(8,128)(2,1)S(1)}, u32[]{:S(2)}, u32[]{:S(2)}) collective-permute-start(bf16[4,32,128]{2,1,0:T(8,128)(2,1)S(1)} %pairs_summed.1.refs_0_), channel_id=1, source_target_pairs={{0,128},{64,192},{128,0},{192,64},{1,129},{65,193},{129,1},{193,65... | collective-permute-start | bytes 98312 | tf_op jit(solution)/shard_map/ppermute | solution.py:551
  169.1 4.9 %collective-permute-start.27 = (bf16[4,32,128]{2,1,0:T(8,128)(2,1)S(1)}, bf16[4,32,128]{2,1,0:T(8,128)(2,1)S(1)}, u32[]{:S(2)}, u32[]{:S(2)}) collective-permute-start(bf16[4,32,128]{2,1,0:T(8,128)(2,1)S(1)} %pairs_summed.1.refs_0_), channel_id=1, source_target_pairs={{0,192},{64,128},{128,64},{192,0},{1,193},{65,129},{129,65},{193,1... | collective-permute-start | bytes 98312 | tf_op jit(solution)/shard_map/ppermute | solution.py:551
  175.6 20.9 %all-to-all-start.3 = ((bf16[8,2,4,32,128]{4,3,2,1,0:T(8,128)(2,1)}), bf16[8,2,4,32,128]{4,3,2,1,0:T(8,128)(2,1)S(1)}, u32[]{:S(2)}, u32[]{:S(2)}) async-start(bf16[8,2,4,32,128]{4,3,2,1,0:T(8,128)(2,1)} %route.1), calls=%async_computation.3 | async-start | bytes 1048576 | tf_op jit(solution)/shard_map/all_to_all | solution.py:472
  180.5 14.3 %collective-permute-start.22 = (bf16[128,512]{1,0:T(8,128)(2,1)S(1)}, bf16[128,512]{1,0:T(8,128)(2,1)S(1)}, u32[]{:S(2)}, u32[]{:S(2)}) collective-permute-start(bf16[128,512]{1,0:T(8,128)(2,1)S(1)} %get-tuple-element.35), channel_id=1, source_target_pairs={{0,48},{16,0},{32,16},{48,32},{1,49},{17,1},{33,17},{49,33},{2,50}... | collective-permute-start | bytes 393224 | tf_op jit(solution)/shard_map/ppermute | solution.py:466
  180.9 13.9 %collective-permute-start.23 = (bf16[128,512]{1,0:T(8,128)(2,1)S(1)}, bf16[128,512]{1,0:T(8,128)(2,1)S(1)}, u32[]{:S(2)}, u32[]{:S(2)}) collective-permute-start(bf16[128,512]{1,0:T(8,128)(2,1)S(1)} %get-tuple-element.36), channel_id=1, source_target_pairs={{0,32},{16,48},{32,0},{48,16},{1,33},{17,49},{33,1},{49,17},{2,34}... | collective-permute-start | bytes 393224 | tf_op jit(solution)/shard_map/ppermute | solution.py:466
  184.5 11.1 %collective-permute-start.24 = (bf16[128,512]{1,0:T(8,128)(2,1)S(1)}, bf16[128,512]{1,0:T(8,128)(2,1)S(1)}, u32[]{:S(2)}, u32[]{:S(2)}) collective-permute-start(bf16[128,512]{1,0:T(8,128)(2,1)S(1)} %get-tuple-element.37), channel_id=1, source_target_pairs={{0,16},{16,32},{32,48},{48,0},{1,17},{17,33},{33,49},{49,1},{2,18}... | collective-permute-start | bytes 393224 | tf_op jit(solution)/shard_map/ppermute | solution.py:466

commit v2 on v1

--- a/solution.py
+++ b/solution.py
@@ -384,21 +384,24 @@
     parts, out_ref = refs[:4], refs[4]
     dp = lax.axis_index("dp")
     first = (lax.axis_index("zh") * 2 + lax.axis_index("zl")) * 16
-    tasks = [tasks_ref[dp ^ d] for d in range(4)]
-    for h in range(KVH):
-        examples = [part[h].astype(jnp.float32) for part in parts]
-        for r in range(8):
-            for j in range(2):
-                total = jnp.zeros(examples[0].shape, jnp.float32)
-                for d in range(4):
-                    total += jnp.where(tasks[d] == first + r * 2 + j, examples[d], 0.0)
-                out_ref[r, j, h] = total.astype(jnp.bfloat16)
+    places = [tasks_ref[dp ^ d] - first for d in range(4)]
+    here = [(place >= 0) & (place < 16) for place in places]
+    out_ref[...] = jnp.zeros_like(out_ref)
+    for d in range(4):
+
+        @pl.when(here[d])
+        def _():
+            total = parts[d][...].astype(jnp.float32)
+            for e in range(d):
+                same = here[e] & (places[e] == places[d])
+                total += jnp.where(same, parts[e][...].astype(jnp.float32), 0.0)
+            out_ref[jnp.clip(places[d], 0, 15)] = total.astype(jnp.bfloat16)
 
 
 def route(tasks, parts):
     return pl.pallas_call(
         route_kernel,
-        out_shape=jax.ShapeDtypeStruct((8, 2, KVH, 32, HD), jnp.bfloat16),
+        out_shape=jax.ShapeDtypeStruct((16, KVH, 32, HD), jnp.bfloat16),
         in_specs=[SMEM] + [VMEM] * 4,
         out_specs=VMEM,
         compiler_params=params(),
@@ -412,7 +415,8 @@
         rows = slice(r % 4 * 32, r % 4 * 32 + 32)
         for j in range(2):
             for h in range(KVH):
-                out_ref[j, rows, h * HD : (h + 1) * HD] = banks_ref[r, j, h].astype(jnp.float32)
+                part = banks_ref[2 * r + j, h].astype(jnp.float32)
+                out_ref[j, rows, h * HD : (h + 1) * HD] = part
 
 
 def banks_out(banks):

time: 200 us -> 200 us (level)
  no operation moved by 1% of the time
where the time goes in v2:
time: 200 us; the launch traced here: 197 us
  waiting for transfers between devices  71.2 us (36%)
  blocking collectives  48.8 us (24%)
  starting transfers between devices  41.9 us (21%)
  Pallas kernels  34 us (17%)
    all_to_all x3, blocking collectives, exchange(): return lax.all_to_all(blocks, axes, 0, 0, tiled=True)  48.8 us
    ppermute x12, waiting for transfers between devices, turned(): lax.ppermute(parts[d], 'zh', [(i, (i + sign * d) % 4) for i in range(4)])  40.5 us
    ppermute x12, starting transfers between devices, turned(): lax.ppermute(parts[d], 'zh', [(i, (i + sign * d) % 4) for i in range(4)])  19.2 us
    pallas_call x1, Pallas kernels, attend_last(): pl.pallas_call(lambda *refs: last_kernel(names, *refs), out_shape=[jax.Sh...  13.9 us
    ppermute x1, waiting for transfers between devices, step(): far = lax.ppermute(prompt, 'x', [(i, (i + 2) % 4) for i in range(4)])  12.9 us
    pallas_call x1, Pallas kernels, attend_first(): pl.pallas_call(lambda *refs: first_kernel(names, *refs), out_shape=jax.Sh...  11.6 us
    ppermute x1, waiting for transfers between devices, step(): both = lax.ppermute(prompt, ('zl', 'y'), [(i, 3 - i) for i in range(4)])  5.23 us
    ppermute x3, waiting for transfers between devices, step(): parts.append(lax.ppermute(mine, 'dp', [(i, i ^ d) for i in range(4)]))  4.86 us
  transfers between devices with their start and end apart: 29, of which 15 were waited for; matrix products, arithmetic and copies ran while one was open for 0% of the time, Pallas kernels for 8%

profile of v2, /device:TPU:2, one launch (start us, length us, event | category | flops | bytes accessed | tf_op | source)
XLA Modules:
  0.0 197.3 jit_solution(8295026093004799684)
XLA Ops:
  1.8 26.5 %all_to_all.20.refs_4_.refs_9_ = bf16[8,272,128]{2,1,0:T(8,128)(2,1)S(1)} all-to-all(bf16[8,272,128]{2,1,0:T(8,128)(2,1)S(1)} %keys_payload.1), channel_id=1, replica_groups=mesh['dp'=4,'zh'=4,'zl'=2,'x'=4,'y'=2] {'zh','zl'}, dimensions={0} | all-to-all | bytes 1114112 | tf_op jit(solution)/shard_map/all_to_all | solution.py:476
  28.3 1.6 collective-permute-start.6
  29.8 1.5 collective-permute-start.7
  32.5 2.2 %rows_payload.1 = (bf16[128,512]{1,0:T(8,128)(2,1)S(1)}, bf16[128,512]{1,0:T(8,128)(2,1)S(1)}, bf16[128,512]{1,0:T(8,128)(2,1)S(1)}, bf16[128,512]{1,0:T(8,128)(...) custom-call(s32[4]{0:T(128)S(1)} %copy-done, ...), custom_call_target="tpu_custom_call" | custom-call | tf_op jit(solution)/shard_map/rows_payload/pallas_call | solution.py:122
  35.4 3.5 %collective-permute-start.11 = (bf16[64,512]{1,0:T(8,128)(2,1)S(1)}, bf16[64,512]{1,0:T(8,128)(2,1)S(1)}, u32[]{:S(2)}, u32[]{:S(2)}) collective-permute-start(bf16[64,512]{1,0:T(8,128)(2,1)S(1)} %get-tuple-element.33), channel_id=1, source_target_pairs={{0,48},{16,0},{32,16},{48,32},{1,49},{17,1},{33,17},{49,33},{2,50}... | collective-permute-start | bytes 196616 | tf_op jit(solution)/shard_map/ppermute | solution.py:470
  38.9 4.3 %collective-permute-done.10.refs_3_ = bf16[64,512]{1,0:T(8,128)(2,1)S(1)} collective-permute-done((bf16[64,512]{1,0:T(8,128)(2,1)S(1)}, bf16[64,512]{1,0:T(8,128)(2,1)S(1)}, u32[]{:S(2)}, u32[]{:S(2)}) %collective-permute-start.10) | collective-permute-done | bytes 65568 | tf_op jit(solution)/shard_map/ppermute | solution.py:470
  43.7 6.4 %collective-permute-done.9.refs_2_ = bf16[64,512]{1,0:T(8,128)(2,1)S(1)} collective-permute-done((bf16[64,512]{1,0:T(8,128)(2,1)S(1)}, bf16[64,512]{1,0:T(8,128)(2,1)S(1)}, u32[]{:S(2)}, u32[]{:S(2)}) %collective-permute-start.9) | collective-permute-done | bytes 65568 | tf_op jit(solution)/shard_map/ppermute | solution.py:470
  52.0 3.1 %collective-permute-done.12.refs_2_ = bf16[64,512]{1,0:T(8,128)(2,1)S(1)} collective-permute-done((bf16[64,512]{1,0:T(8,128)(2,1)S(1)}, bf16[64,512]{1,0:T(8,128)(2,1)S(1)}, u32[]{:S(2)}, u32[]{:S(2)}) %collective-permute-start.12) | collective-permute-done | bytes 65568 | tf_op jit(solution)/shard_map/ppermute | solution.py:450
  56.0 5.2 %collective-permute-done.14.refs_4_ = bf16[64,512]{1,0:T(8,128)(2,1)S(1)} collective-permute-done((bf16[64,512]{1,0:T(8,128)(2,1)S(1)}, bf16[64,512]{1,0:T(8,128)(2,1)S(1)}, u32[]{:S(2)}, u32[]{:S(2)}) %collective-permute-start.14) | collective-permute-done | bytes 65568 | tf_op jit(solution)/shard_map/ppermute | solution.py:529
  61.2 1.2 collective-permute-start.1
  63.7 9.6 %collective-permute-done.1.refs_2_ = bf16[128,512]{1,0:T(8,128)(2,1)S(1)} collective-permute-done((bf16[128,512]{1,0:T(8,128)(2,1)S(1)}, bf16[128,512]{1,0:T(8,128)(2,1)S(1)}, u32[]{:S(2)}, u32[]{:S(2)}) %collective-permute-start.1) | collective-permute-done | bytes 131104 | tf_op jit(solution)/shard_map/ppermute | solution.py:470
  73.9 1.6 collective-permute-start.15
  75.5 1.2 collective-permute-start.19
  76.7 3.7 %collective-permute-done.3.refs_5_ = bf16[128,512]{1,0:T(8,128)(2,1)S(1)} collective-permute-done((bf16[128,512]{1,0:T(8,128)(2,1)S(1)}, bf16[128,512]{1,0:T(8,128)(2,1)S(1)}, u32[]{:S(2)}, u32[]{:S(2)}) %collective-permute-start.3) | collective-permute-done | bytes 131104 | tf_op jit(solution)/shard_map/ppermute | solution.py:470
  80.4 1.7 collective-permute-start.20
  82.9 2.9 %collective-permute-start.16 = (bf16[64,512]{1,0:T(8,128)(2,1)S(1)}, bf16[64,512]{1,0:T(8,128)(2,1)S(1)}, u32[]{:S(2)}, u32[]{:S(2)}) collective-permute-start(bf16[64,512]{1,0:T(8,128)(2,1)S(1)} %shard_map.104.refs_1_), channel_id=1, source_target_pairs={{0,4},{2,6},{4,0},{6,2},{1,5},{3,7},{5,1},{7,3},{8,12},{10,14},{12... | collective-permute-start | bytes 196616 | tf_op jit(solution)/shard_map/ppermute | solution.py:533
  85.8 12.9 %collective-permute-done.16.refs_3_ = bf16[64,512]{1,0:T(8,128)(2,1)S(1)} collective-permute-done((bf16[64,512]{1,0:T(8,128)(2,1)S(1)}, bf16[64,512]{1,0:T(8,128)(2,1)S(1)}, u32[]{:S(2)}, u32[]{:S(2)}) %collective-permute-start.16) | collective-permute-done | bytes 65568 | tf_op jit(solution)/shard_map/ppermute | solution.py:533
  98.7 4.3 %collective-permute-done.17.refs_4_ = bf16[64,512]{1,0:T(8,128)(2,1)S(1)} collective-permute-done((bf16[64,512]{1,0:T(8,128)(2,1)S(1)}, bf16[64,512]{1,0:T(8,128)(2,1)S(1)}, u32[]{:S(2)}, u32[]{:S(2)}) %collective-permute-start.17) | collective-permute-done | bytes 65568 | tf_op jit(solution)/shard_map/ppermute | solution.py:458
  103.0 3.7 %collective-permute-start.4 = (bf16[128,512]{1,0:T(8,128)(2,1)S(1)}, bf16[128,512]{1,0:T(8,128)(2,1)S(1)}, u32[]{:S(2)}, u32[]{:S(2)}) collective-permute-start(bf16[128,512]{1,0:T(8,128)(2,1)S(1)} %get-tuple-element.28), channel_id=1, source_target_pairs={{0,32},{16,48},{32,0},{48,16},{1,33},{17,49},{33,1},{49,17},{2,34}... | collective-permute-start | bytes 393224 | tf_op jit(solution)/shard_map/ppermute | solution.py:470
  107.2 4.7 %collective-permute-done.4.refs_6_ = bf16[128,512]{1,0:T(8,128)(2,1)S(1)} collective-permute-done((bf16[128,512]{1,0:T(8,128)(2,1)S(1)}, bf16[128,512]{1,0:T(8,128)(2,1)S(1)}, u32[]{:S(2)}, u32[]{:S(2)}) %collective-permute-start.4) | collective-permute-done | bytes 131104 | tf_op jit(solution)/shard_map/ppermute | solution.py:470
  111.9 5.0 %collective-permute-start.5 = (bf16[128,512]{1,0:T(8,128)(2,1)S(1)}, bf16[128,512]{1,0:T(8,128)(2,1)S(1)}, u32[]{:S(2)}, u32[]{:S(2)}) collective-permute-start(bf16[128,512]{1,0:T(8,128)(2,1)S(1)} %get-tuple-element.29), channel_id=1, source_target_pairs={{0,48},{16,0},{32,16},{48,32},{1,49},{17,1},{33,17},{49,33},{2,50}... | collective-permute-start | bytes 393224 | tf_op jit(solution)/shard_map/ppermute | solution.py:470
  116.9 11.6 %attend_first.1.refs_8_ = f32[4,512,256]{2,1,0:T(8,128)S(1)} custom-call(bf16[128,512]{1,0:T(8,128)(2,1)S(1)} %get-tuple-element.22.refs_0_, bf16[128,512]{1,0:T(8,128)(2,1)S(1)} %collective-permute-done.refs_1_, bf16[128,512]{1,0:T(8,128)(2,1)S(1)} %collective-permute-done.1.refs_2_, bf16[128,512]{1,0:T(8,128)(2,1)S(1)} %collective-permute-done.2.refs_3_, ...), custom_call_target="tpu_custom_call" | custom-call | flops 2684354560 | bytes 4194304 | tf_op jit(solution)/shard_map/attend_first/pallas_call | solution.py:243
  128.6 13.9 %attend_last.1 = (bf16[128,512]{1,0:T(8,128)(2,1)S(1)}, bf16[128,512]{1,0:T(8,128)(2,1)S(1)}, bf16[128,512]{1,0:T(8,128)(2,1)S(1)}, bf16[128,512]{1,0:T(8,128)(2,1)S(1)}, bf16[256,128]{1,0:T(8,128)(2,1)S(1)}) custom-call(bf16[128,512]{1,0:T(8,128)(2,1)S(1)} %get-tuple-element.22.refs_0_, bf16[128,512]{1,0:T(8,128)(2,1)S(1)} %collective-permute-done.refs_1_, ...), custom_call_target="tpu_custom_call" | custom-call | flops 3355443200 | bytes 4194304 | tf_op jit(solution)/shard_map/attend_last/pallas_call | solution.py:323
  142.5 10.7 %all_to_all.21.pieces_ref = bf16[8,32,128]{2,1,0:T(8,128)(2,1)S(1)} all-to-all(bf16[8,32,128]{2,1,0:T(8,128)(2,1)S(1)} %bitcast.1), channel_id=1, replica_groups=mesh['dp'=4,'zh'=4,'zl'=2,'x'=4,'y'=2] {'x','y'}, dimensions={0} | all-to-all | bytes 131072 | tf_op jit(solution)/shard_map/all_to_all | solution.py:476
  153.2 11.7 %all_to_all.22.sent_ref = bf16[8,32,128]{2,1,0:T(8,128)(2,1)S(1)} all-to-all(bf16[8,32,128]{2,1,0:T(8,128)(2,1)S(1)} %summed.1), channel_id=1, replica_groups=mesh['dp'=4,'zh'=4,'zl'=2,'x'=4,'y'=2] {'zh','zl'}, dimensions={0} | all-to-all | bytes 131072 | tf_op jit(solution)/shard_map/all_to_all | solution.py:476
  165.0 4.1 %collective-permute-start.26 = (bf16[4,32,128]{2,1,0:T(8,128)(2,1)S(1)}, bf16[4,32,128]{2,1,0:T(8,128)(2,1)S(1)}, u32[]{:S(2)}, u32[]{:S(2)}) collective-permute-start(bf16[4,32,128]{2,1,0:T(8,128)(2,1)S(1)} %pairs_summed.1.refs_0_), channel_id=1, source_target_pairs={{0,128},{64,192},{128,0},{192,64},{1,129},{65,193},{129,1},{193,65... | collective-permute-start | bytes 98312 | tf_op jit(solution)/shard_map/ppermute | solution.py:555
  169.1 1.9 collective-permute-done.26.refs_2_
  171.0 2.9 %collective-permute-done.27.refs_3_ = bf16[4,32,128]{2,1,0:T(8,128)(2,1)S(1)} collective-permute-done((bf16[4,32,128]{2,1,0:T(8,128)(2,1)S(1)}, bf16[4,32,128]{2,1,0:T(8,128)(2,1)S(1)}, u32[]{:S(2)}, u32[]{:S(2)}) %collective-permute-start.27) | collective-permute-done | bytes 32800 | tf_op jit(solution)/shard_map/ppermute | solution.py:555
  174.0 1.4 route.1
  175.4 4.9 %all-to-all-start.3 = ((bf16[16,4,32,128]{3,2,1,0:T(8,128)(2,1)}), bf16[16,4,32,128]{3,2,1,0:T(8,128)(2,1)S(1)}, u32[]{:S(2)}, u32[]{:S(2)}) async-start(bf16[16,4,32,128]{3,2,1,0:T(8,128)(2,1)} %route.1), calls=%async_computation.3 | async-start | bytes 1048576 | tf_op jit(solution)/shard_map/all_to_all | solution.py:476
  180.6 3.7 %collective-permute-start.23 = (bf16[128,512]{1,0:T(8,128)(2,1)S(1)}, bf16[128,512]{1,0:T(8,128)(2,1)S(1)}, u32[]{:S(2)}, u32[]{:S(2)}) collective-permute-start(bf16[128,512]{1,0:T(8,128)(2,1)S(1)} %get-tuple-element.36), channel_id=1, source_target_pairs={{0,32},{16,48},{32,0},{48,16},{1,33},{17,49},{33,1},{49,17},{2,34}... | collective-permute-start | bytes 393224 | tf_op jit(solution)/shard_map/ppermute | solution.py:470
  184.3 10.2 %collective-permute-done.22.refs_1_ = bf16[128,512]{1,0:T(8,128)(2,1)S(1)} collective-permute-done((bf16[128,512]{1,0:T(8,128)(2,1)S(1)}, bf16[128,512]{1,0:T(8,128)(2,1)S(1)}, u32[]{:S(2)}, u32[]{:S(2)}) %collective-permute-start.22) | collective-permute-done | bytes 131104 | tf_op jit(solution)/shard_map/ppermute | solution.py:470
  (45 shorter events, 12.8 us)
Async XLA Ops:
  28.3 47.2 %collective-permute-start.6 = (bf16[8,272,128]{2,1,0:T(8,128)(2,1)S(1)}, bf16[8,272,128]{2,1,0:T(8,128)(2,1)S(1)}, u32[]{:S(2)}, u32[]{:S(2)}) collective-permute-start(bf16[8,272,128]{2,1,0:T(8,128)(2,1)S(1)} %all_to_all.20.refs_4_.refs_9_), channel_id=1, source_target_pairs={{0,1},{1,0},{2,3},{3,2},{4,5},{5,4},{6,7},{7,6},{8,9},{9,8},{10,11... | collective-permute-start | bytes 1671176 | tf_op jit(solution)/shard_map/ppermute | solution.py:450
  29.8 52.3 %collective-permute-start.7 = (bf16[8,272,128]{2,1,0:T(8,128)(2,1)S(1)}, bf16[8,272,128]{2,1,0:T(8,128)(2,1)S(1)}, u32[]{:S(2)}, u32[]{:S(2)}) collective-permute-start(bf16[8,272,128]{2,1,0:T(8,128)(2,1)S(1)} %all_to_all.20.refs_4_.refs_9_), channel_id=1, source_target_pairs={{0,2},{2,4},{4,6},{6,0},{1,3},{3,5},{5,7},{7,1},{8,10},{10,12},{12... | collective-permute-start | bytes 1671176 | tf_op jit(solution)/shard_map/ppermute | solution.py:454
  31.3 51.1 %collective-permute-start.8 = (bf16[8,272,128]{2,1,0:T(8,128)(2,1)S(1)}, bf16[8,272,128]{2,1,0:T(8,128)(2,1)S(1)}, u32[]{:S(2)}, u32[]{:S(2)}) collective-permute-start(bf16[8,272,128]{2,1,0:T(8,128)(2,1)S(1)} %all_to_all.20.refs_4_.refs_9_), channel_id=1, source_target_pairs={{0,6},{2,0},{4,2},{6,4},{1,7},{3,1},{5,3},{7,5},{8,14},{10,8},{12,... | collective-permute-start | bytes 1671176 | tf_op jit(solution)/shard_map/ppermute | solution.py:458
  31.9 0.7 copy-start
  34.7 8.4 %collective-permute-start.10 = (bf16[64,512]{1,0:T(8,128)(2,1)S(1)}, bf16[64,512]{1,0:T(8,128)(2,1)S(1)}, u32[]{:S(2)}, u32[]{:S(2)}) collective-permute-start(bf16[64,512]{1,0:T(8,128)(2,1)S(1)} %get-tuple-element.32), channel_id=1, source_target_pairs={{0,32},{16,48},{32,0},{48,16},{1,33},{17,49},{33,1},{49,17},{2,34}... | collective-permute-start | bytes 196616 | tf_op jit(solution)/shard_map/ppermute | solution.py:470
  35.4 8.3 %collective-permute-start.11 = (bf16[64,512]{1,0:T(8,128)(2,1)S(1)}, bf16[64,512]{1,0:T(8,128)(2,1)S(1)}, u32[]{:S(2)}, u32[]{:S(2)}) collective-permute-start(bf16[64,512]{1,0:T(8,128)(2,1)S(1)} %get-tuple-element.33), channel_id=1, source_target_pairs={{0,48},{16,0},{32,16},{48,32},{1,49},{17,1},{33,17},{49,33},{2,50}... | collective-permute-start | bytes 196616 | tf_op jit(solution)/shard_map/ppermute | solution.py:470
  43.2 7.0 %collective-permute-start.9 = (bf16[64,512]{1,0:T(8,128)(2,1)S(1)}, bf16[64,512]{1,0:T(8,128)(2,1)S(1)}, u32[]{:S(2)}, u32[]{:S(2)}) collective-permute-start(bf16[64,512]{1,0:T(8,128)(2,1)S(1)} %get-tuple-element.31), channel_id=1, source_target_pairs={{0,16},{16,32},{32,48},{48,0},{1,17},{17,33},{33,49},{49,1},{2,18}... | collective-permute-start | bytes 196616 | tf_op jit(solution)/shard_map/ppermute | solution.py:470
  50.7 4.4 %collective-permute-start.12 = (bf16[64,512]{1,0:T(8,128)(2,1)S(1)}, bf16[64,512]{1,0:T(8,128)(2,1)S(1)}, u32[]{:S(2)}, u32[]{:S(2)}) collective-permute-start(bf16[64,512]{1,0:T(8,128)(2,1)S(1)} %shard_map.103.refs_1_), channel_id=1, source_target_pairs={{0,1},{1,0},{2,3},{3,2},{4,5},{5,4},{6,7},{7,6},{8,9},{9,8},{10,11... | collective-permute-start | bytes 196616 | tf_op jit(solution)/shard_map/ppermute | solution.py:450
  51.7 4.3 %collective-permute-start.13 = (bf16[64,512]{1,0:T(8,128)(2,1)S(1)}, bf16[64,512]{1,0:T(8,128)(2,1)S(1)}, u32[]{:S(2)}, u32[]{:S(2)}) collective-permute-start(bf16[64,512]{1,0:T(8,128)(2,1)S(1)} %shard_map.103.refs_1_), channel_id=1, source_target_pairs={{0,8},{8,0},{1,9},{9,1},{2,10},{10,2},{3,11},{11,3},{4,12},{12,4},... | collective-permute-start | bytes 196616 | tf_op jit(solution)/shard_map/ppermute | solution.py:450
  55.1 6.1 %collective-permute-start.14 = (bf16[64,512]{1,0:T(8,128)(2,1)S(1)}, bf16[64,512]{1,0:T(8,128)(2,1)S(1)}, u32[]{:S(2)}, u32[]{:S(2)}) collective-permute-start(bf16[64,512]{1,0:T(8,128)(2,1)S(1)} %shard_map.103.refs_1_), channel_id=1, source_target_pairs={{0,9},{1,8},{8,1},{9,0},{2,11},{3,10},{10,3},{11,2},{4,13},{5,12},... | collective-permute-start | bytes 196616 | tf_op jit(solution)/shard_map/ppermute | solution.py:529
  56.0 7.2 %collective-permute-start = (bf16[128,512]{1,0:T(8,128)(2,1)S(1)}, bf16[128,512]{1,0:T(8,128)(2,1)S(1)}, u32[]{:S(2)}, u32[]{:S(2)}) collective-permute-start(bf16[128,512]{1,0:T(8,128)(2,1)S(1)} %get-tuple-element.23), channel_id=1, source_target_pairs={{0,16},{16,32},{32,48},{48,0},{1,17},{17,33},{33,49},{49,1},{2,18}... | collective-permute-start | bytes 393224 | tf_op jit(solution)/shard_map/ppermute | solution.py:470
  61.2 12.1 %collective-permute-start.1 = (bf16[128,512]{1,0:T(8,128)(2,1)S(1)}, bf16[128,512]{1,0:T(8,128)(2,1)S(1)}, u32[]{:S(2)}, u32[]{:S(2)}) collective-permute-start(bf16[128,512]{1,0:T(8,128)(2,1)S(1)} %get-tuple-element.24), channel_id=1, source_target_pairs={{0,32},{16,48},{32,0},{48,16},{1,33},{17,49},{33,1},{49,17},{2,34}... | collective-permute-start | bytes 393224 | tf_op jit(solution)/shard_map/ppermute | solution.py:470
  63.1 10.8 %collective-permute-start.2 = (bf16[128,512]{1,0:T(8,128)(2,1)S(1)}, bf16[128,512]{1,0:T(8,128)(2,1)S(1)}, u32[]{:S(2)}, u32[]{:S(2)}) collective-permute-start(bf16[128,512]{1,0:T(8,128)(2,1)S(1)} %get-tuple-element.25), channel_id=1, source_target_pairs={{0,48},{16,0},{32,16},{48,32},{1,49},{17,1},{33,17},{49,33},{2,50}... | collective-permute-start | bytes 393224 | tf_op jit(solution)/shard_map/ppermute | solution.py:470
  73.3 7.1 %collective-permute-start.3 = (bf16[128,512]{1,0:T(8,128)(2,1)S(1)}, bf16[128,512]{1,0:T(8,128)(2,1)S(1)}, u32[]{:S(2)}, u32[]{:S(2)}) collective-permute-start(bf16[128,512]{1,0:T(8,128)(2,1)S(1)} %get-tuple-element.27), channel_id=1, source_target_pairs={{0,16},{16,32},{32,48},{48,0},{1,17},{17,33},{33,49},{49,1},{2,18}... | collective-permute-start | bytes 393224 | tf_op jit(solution)/shard_map/ppermute | solution.py:470
  73.9 9.0 %collective-permute-start.15 = (bf16[64,512]{1,0:T(8,128)(2,1)S(1)}, bf16[64,512]{1,0:T(8,128)(2,1)S(1)}, u32[]{:S(2)}, u32[]{:S(2)}) collective-permute-start(bf16[64,512]{1,0:T(8,128)(2,1)S(1)} %shard_map.104.refs_1_), channel_id=1, source_target_pairs={{0,2},{2,4},{4,6},{6,0},{1,3},{3,5},{5,7},{7,1},{8,10},{10,12},{12... | collective-permute-start | bytes 196616 | tf_op jit(solution)/shard_map/ppermute | solution.py:454
  75.5 53.0 %collective-permute-start.19 = (bf16[8,272,128]{2,1,0:T(8,128)(2,1)S(1)}, bf16[8,272,128]{2,1,0:T(8,128)(2,1)S(1)}, u32[]{:S(2)}, u32[]{:S(2)}) collective-permute-start(bf16[8,272,128]{2,1,0:T(8,128)(2,1)S(1)} %collective-permute-done.6.refs_5_), channel_id=1, source_target_pairs={{0,2},{2,4},{4,6},{6,0},{1,3},{3,5},{5,7},{7,1},{8,10},{10,12},{12... | collective-permute-start | bytes 1671176 | tf_op jit(solution)/shard_map/ppermute | solution.py:454
  80.4 48.2 %collective-permute-start.20 = (bf16[8,272,128]{2,1,0:T(8,128)(2,1)S(1)}, bf16[8,272,128]{2,1,0:T(8,128)(2,1)S(1)}, u32[]{:S(2)}, u32[]{:S(2)}) collective-permute-start(bf16[8,272,128]{2,1,0:T(8,128)(2,1)S(1)} %collective-permute-done.6.refs_5_), channel_id=1, source_target_pairs={{0,6},{2,0},{4,2},{6,4},{1,7},{3,1},{5,3},{7,5},{8,14},{10,8},{12,... | collective-permute-start | bytes 1671176 | tf_op jit(solution)/shard_map/ppermute | solution.py:458
  82.1 46.4 %collective-permute-start.18 = (bf16[8,272,128]{2,1,0:T(8,128)(2,1)S(1)}, bf16[8,272,128]{2,1,0:T(8,128)(2,1)S(1)}, u32[]{:S(2)}, u32[]{:S(2)}) collective-permute-start(bf16[8,272,128]{2,1,0:T(8,128)(2,1)S(1)} %collective-permute-done.7.refs_6_), channel_id=1, source_target_pairs={{0,2},{2,4},{4,6},{6,0},{1,3},{3,5},{5,7},{7,1},{8,10},{10,12},{12... | collective-permute-start | bytes 1671176 | tf_op jit(solution)/shard_map/ppermute | solution.py:454
  82.4 46.1 %collective-permute-start.21 = (bf16[8,272,128]{2,1,0:T(8,128)(2,1)S(1)}, bf16[8,272,128]{2,1,0:T(8,128)(2,1)S(1)}, u32[]{:S(2)}, u32[]{:S(2)}) collective-permute-start(bf16[8,272,128]{2,1,0:T(8,128)(2,1)S(1)} %collective-permute-done.8.refs_7_), channel_id=1, source_target_pairs={{0,7},{1,6},{2,1},{3,0},{4,3},{5,2},{6,5},{7,4},{8,15},{9,14},{10,... | collective-permute-start | bytes 1671176 | tf_op jit(solution)/shard_map/ppermute | solution.py:463
  82.9 15.8 %collective-permute-start.16 = (bf16[64,512]{1,0:T(8,128)(2,1)S(1)}, bf16[64,512]{1,0:T(8,128)(2,1)S(1)}, u32[]{:S(2)}, u32[]{:S(2)}) collective-permute-start(bf16[64,512]{1,0:T(8,128)(2,1)S(1)} %shard_map.104.refs_1_), channel_id=1, source_target_pairs={{0,4},{2,6},{4,0},{6,2},{1,5},{3,7},{5,1},{7,3},{8,12},{10,14},{12... | collective-permute-start | bytes 196616 | tf_op jit(solution)/shard_map/ppermute | solution.py:533
  98.7 4.3 %collective-permute-start.17 = (bf16[64,512]{1,0:T(8,128)(2,1)S(1)}, bf16[64,512]{1,0:T(8,128)(2,1)S(1)}, u32[]{:S(2)}, u32[]{:S(2)}) collective-permute-start(bf16[64,512]{1,0:T(8,128)(2,1)S(1)} %shard_map.104.refs_1_), channel_id=1, source_target_pairs={{0,6},{2,0},{4,2},{6,4},{1,7},{3,1},{5,3},{7,5},{8,14},{10,8},{12,... | collective-permute-start | bytes 196616 | tf_op jit(solution)/shard_map/ppermute | solution.py:458
  103.0 8.9 %collective-permute-start.4 = (bf16[128,512]{1,0:T(8,128)(2,1)S(1)}, bf16[128,512]{1,0:T(8,128)(2,1)S(1)}, u32[]{:S(2)}, u32[]{:S(2)}) collective-permute-start(bf16[128,512]{1,0:T(8,128)(2,1)S(1)} %get-tuple-element.28), channel_id=1, source_target_pairs={{0,32},{16,48},{32,0},{48,16},{1,33},{17,49},{33,1},{49,17},{2,34}... | collective-permute-start | bytes 393224 | tf_op jit(solution)/shard_map/ppermute | solution.py:470
  111.9 16.6 %collective-permute-start.5 = (bf16[128,512]{1,0:T(8,128)(2,1)S(1)}, bf16[128,512]{1,0:T(8,128)(2,1)S(1)}, u32[]{:S(2)}, u32[]{:S(2)}) collective-permute-start(bf16[128,512]{1,0:T(8,128)(2,1)S(1)} %get-tuple-element.29), channel_id=1, source_target_pairs={{0,48},{16,0},{32,16},{48,32},{1,49},{17,1},{33,17},{49,33},{2,50}... | collective-permute-start | bytes 393224 | tf_op jit(solution)/shard_map/ppermute | solution.py:470
  128.6 45.4 %copy-start.1 = (s32[4]{0:T(128)S(1)}, s32[4]{0:T(128)}, u32[]{:S(2)}) copy-start(s32[4]{0:T(128)} %tasks_ref.3) | copy-start | bytes 52
  164.9 4.2 %collective-permute-start.25 = (bf16[4,32,128]{2,1,0:T(8,128)(2,1)S(1)}, bf16[4,32,128]{2,1,0:T(8,128)(2,1)S(1)}, u32[]{:S(2)}, u32[]{:S(2)}) collective-permute-start(bf16[4,32,128]{2,1,0:T(8,128)(2,1)S(1)} %pairs_summed.1.refs_0_), channel_id=1, source_target_pairs={{0,64},{64,0},{128,192},{192,128},{1,65},{65,1},{129,193},{193,129... | collective-permute-start | bytes 98312 | tf_op jit(solution)/shard_map/ppermute | solution.py:555
  165.0 6.0 %collective-permute-start.26 = (bf16[4,32,128]{2,1,0:T(8,128)(2,1)S(1)}, bf16[4,32,128]{2,1,0:T(8,128)(2,1)S(1)}, u32[]{:S(2)}, u32[]{:S(2)}) collective-permute-start(bf16[4,32,128]{2,1,0:T(8,128)(2,1)S(1)} %pairs_summed.1.refs_0_), channel_id=1, source_target_pairs={{0,128},{64,192},{128,0},{192,64},{1,129},{65,193},{129,1},{193,65... | collective-permute-start | bytes 98312 | tf_op jit(solution)/shard_map/ppermute | solution.py:555
  169.1 4.9 %collective-permute-start.27 = (bf16[4,32,128]{2,1,0:T(8,128)(2,1)S(1)}, bf16[4,32,128]{2,1,0:T(8,128)(2,1)S(1)}, u32[]{:S(2)}, u32[]{:S(2)}) collective-permute-start(bf16[4,32,128]{2,1,0:T(8,128)(2,1)S(1)} %pairs_summed.1.refs_0_), channel_id=1, source_target_pairs={{0,192},{64,128},{128,64},{192,0},{1,193},{65,129},{129,65},{193,1... | collective-permute-start | bytes 98312 | tf_op jit(solution)/shard_map/ppermute | solution.py:555
  175.4 20.9 %all-to-all-start.3 = ((bf16[16,4,32,128]{3,2,1,0:T(8,128)(2,1)}), bf16[16,4,32,128]{3,2,1,0:T(8,128)(2,1)S(1)}, u32[]{:S(2)}, u32[]{:S(2)}) async-start(bf16[16,4,32,128]{3,2,1,0:T(8,128)(2,1)} %route.1), calls=%async_computation.3 | async-start | bytes 1048576 | tf_op jit(solution)/shard_map/all_to_all | solution.py:476
  180.3 14.3 %collective-permute-start.22 = (bf16[128,512]{1,0:T(8,128)(2,1)S(1)}, bf16[128,512]{1,0:T(8,128)(2,1)S(1)}, u32[]{:S(2)}, u32[]{:S(2)}) collective-permute-start(bf16[128,512]{1,0:T(8,128)(2,1)S(1)} %get-tuple-element.35), channel_id=1, source_target_pairs={{0,48},{16,0},{32,16},{48,32},{1,49},{17,1},{33,17},{49,33},{2,50}... | collective-permute-start | bytes 393224 | tf_op jit(solution)/shard_map/ppermute | solution.py:470
  180.6 13.9 %collective-permute-start.23 = (bf16[128,512]{1,0:T(8,128)(2,1)S(1)}, bf16[128,512]{1,0:T(8,128)(2,1)S(1)}, u32[]{:S(2)}, u32[]{:S(2)}) collective-permute-start(bf16[128,512]{1,0:T(8,128)(2,1)S(1)} %get-tuple-element.36), channel_id=1, source_target_pairs={{0,32},{16,48},{32,0},{48,16},{1,33},{17,49},{33,1},{49,17},{2,34}... | collective-permute-start | bytes 393224 | tf_op jit(solution)/shard_map/ppermute | solution.py:470
  184.3 11.1 %collective-permute-start.24 = (bf16[128,512]{1,0:T(8,128)(2,1)S(1)}, bf16[128,512]{1,0:T(8,128)(2,1)S(1)}, u32[]{:S(2)}, u32[]{:S(2)}) collective-permute-start(bf16[128,512]{1,0:T(8,128)(2,1)S(1)} %get-tuple-element.37), channel_id=1, source_target_pairs={{0,16},{16,32},{32,48},{48,0},{1,17},{17,33},{33,49},{49,1},{2,18}... | collective-permute-start | bytes 393224 | tf_op jit(solution)/shard_map/ppermute | solution.py:470

commit v3 on v2

--- a/solution.py
+++ b/solution.py
@@ -282,12 +282,13 @@
 
     blocks = range(KVH)
     for d in blocks:
+        scores_ref[d] = dot_nt(q_ref[d], prompt_k)
+    for d in blocks:
         loaded(d).wait()
     for d in blocks:
         acc_ref[d, :, :HD] = state_ref[d, :, :HD]
         acc_ref[d, :, HD:] = jnp.broadcast_to(state_ref[d, :, HD : HD + 1], (GROUP * TOK, HD))
         peak_ref[d] = state_ref[d, :, 2 * HD - 1 :]
-        scores_ref[d] = dot_nt(q_ref[d], prompt_k)
     for d in blocks:
         accumulate(scores_ref[d], prompt_wide, acc_ref.at[d], peak_ref.at[d], slice(None))
 
@@ -477,16 +478,17 @@
 
 
 def choose_kernel(stage, tasks_ref, *refs):
-    parts, out_ref = refs[:KVH], refs[KVH]
+    parts, out_ref = refs[:-1], refs[-1]
     owner = tasks_ref[lax.axis_index("dp")] // 2
     if stage == "zh":
         wanted = (lax.axis_index("zh") + KVH - owner // 16) % KVH
-    elif stage == "zl_y":
-        zl, y = lax.axis_index("zl"), lax.axis_index("y")
-        wanted = ((owner // 8 + zl) % 2) * 2 + (owner + y) % 2
+    elif stage == "zl":
+        wanted = (owner // 8 + lax.axis_index("zl")) % 2
+    elif stage == "y":
+        wanted = (owner + lax.axis_index("y")) % 2
     else:
         wanted = (lax.axis_index("x") + 4 - (owner // 2) % 4) % 4
-    for n in range(KVH):
+    for n in range(len(parts)):
 
         @pl.when(wanted == n)
         def _():
@@ -497,7 +499,7 @@
     return pl.pallas_call(
         lambda *refs: choose_kernel(stage, *refs),
         out_shape=jax.ShapeDtypeStruct(parts[0].shape, parts[0].dtype),
-        in_specs=[SMEM] + [VMEM] * KVH,
+        in_specs=[SMEM] + [VMEM] * len(parts),
         out_specs=VMEM,
         compiler_params=params(4),
     )(tasks, *parts)
@@ -526,10 +528,10 @@
     go = turned(go, 1)
 
     prompt = choose("zh", task_ids, prompts)
-    both = lax.ppermute(prompt, ("zl", "y"), [(i, 3 - i) for i in range(4)])
     flipped = swap(prompt, "zl")
+    prompt = choose("zl", task_ids, (prompt, flipped))
     beyond = swap(prompt, "y")
-    prompt = choose("zl_y", task_ids, (prompt, beyond, flipped, both))
+    prompt = choose("y", task_ids, (prompt, beyond))
     far = lax.ppermute(prompt, "x", [(i, (i + 2) % 4) for i in range(4)])
     prompt_left = from_left(prompt)
     prompt_right = from_right(prompt)

time: 200 us -> 195 us (0.975)
  starting transfers between devices: 41.9 us -> 38.6 us
    ppermute x1 -> x0, waiting for transfers between devices: 5.23 us -> none  [step(): both = lax.ppermute(prompt, ('zl', 'y'), [(i, 3 - i) for i in range(4)])]
    ppermute x1, waiting for transfers between devices: 12.9 us -> 15.4 us  [step(): far = lax.ppermute(prompt, 'x', [(i, (i + 2) % 4) for i in range(4)])]
    ppermute x12, starting transfers between devices: 19.2 us -> 16.7 us  [turned(): lax.ppermute(parts[d], 'zh', [(i, (i + sign * d) % 4) for i in range(4)])]
  transfers between devices with their start and end apart: 29 -> 28, of which waited for: 15 -> 13; matrix products, arithmetic and copies ran while one was open for 0% -> 0% of each run, Pallas kernels for 8% -> 9%
where the time goes in v3:
time: 195 us; the launch traced here: 192 us
  waiting for transfers between devices  70.5 us (36%)
  blocking collectives  47 us (24%)
  starting transfers between devices  38.6 us (20%)
  Pallas kernels  34.7 us (18%)
    all_to_all x3, blocking collectives, exchange(): return lax.all_to_all(blocks, axes, 0, 0, tiled=True)  47 us
    ppermute x12, waiting for transfers between devices, turned(): lax.ppermute(parts[d], 'zh', [(i, (i + sign * d) % 4) for i in range(4)])  42.2 us
    ppermute x12, starting transfers between devices, turned(): lax.ppermute(parts[d], 'zh', [(i, (i + sign * d) % 4) for i in range(4)])  16.7 us
    ppermute x1, waiting for transfers between devices, step(): far = lax.ppermute(prompt, 'x', [(i, (i + 2) % 4) for i in range(4)])  15.4 us
    pallas_call x1, Pallas kernels, attend_last(): pl.pallas_call(lambda *refs: last_kernel(names, *refs), out_shape=[jax.Sh...  14.1 us
    pallas_call x1, Pallas kernels, attend_first(): pl.pallas_call(lambda *refs: first_kernel(names, *refs), out_shape=jax.Sh...  11.6 us
    ppermute x4, starting transfers between devices, from_left(): return lax.ppermute(value, 'x', [(i, (i + 1) % 4) for i in range(4)])  5.38 us
    all_to_all x1, starting transfers between devices, exchange(): return lax.all_to_all(blocks, axes, 0, 0, tiled=True)  4.86 us
  transfers between devices with their start and end apart: 28, of which 13 were waited for; matrix products, arithmetic and copies ran while one was open for 0% of the time, Pallas kernels for 9%

profile of v3, /device:TPU:2, one launch (start us, length us, event | category | flops | bytes accessed | tf_op | source)
XLA Modules:
  0.0 192.3 jit_solution(8096812465859730868)
XLA Ops:
  1.8 26.5 %all_to_all.20.refs_4_.refs_9_ = bf16[8,272,128]{2,1,0:T(8,128)(2,1)S(1)} all-to-all(bf16[8,272,128]{2,1,0:T(8,128)(2,1)S(1)} %keys_payload.1), channel_id=1, replica_groups=mesh['dp'=4,'zh'=4,'zl'=2,'x'=4,'y'=2] {'zh','zl'}, dimensions={0} | all-to-all | bytes 1114112 | tf_op jit(solution)/shard_map/all_to_all | solution.py:477
  28.3 1.6 collective-permute-start.6
  29.8 1.5 collective-permute-start.7
  32.5 2.2 %rows_payload.1 = (bf16[128,512]{1,0:T(8,128)(2,1)S(1)}, bf16[128,512]{1,0:T(8,128)(2,1)S(1)}, bf16[128,512]{1,0:T(8,128)(2,1)S(1)}, bf16[128,512]{1,0:T(8,128)(...) custom-call(s32[4]{0:T(128)S(1)} %copy-done, ...), custom_call_target="tpu_custom_call" | custom-call | tf_op jit(solution)/shard_map/rows_payload/pallas_call | solution.py:122
  35.4 3.5 %collective-permute-start.11 = (bf16[64,512]{1,0:T(8,128)(2,1)S(1)}, bf16[64,512]{1,0:T(8,128)(2,1)S(1)}, u32[]{:S(2)}, u32[]{:S(2)}) collective-permute-start(bf16[64,512]{1,0:T(8,128)(2,1)S(1)} %get-tuple-element.33), channel_id=1, source_target_pairs={{0,48},{16,0},{32,16},{48,32},{1,49},{17,1},{33,17},{49,33},{2,50}... | collective-permute-start | bytes 196616 | tf_op jit(solution)/shard_map/ppermute | solution.py:471
  38.9 4.3 %collective-permute-done.10.refs_3_ = bf16[64,512]{1,0:T(8,128)(2,1)S(1)} collective-permute-done((bf16[64,512]{1,0:T(8,128)(2,1)S(1)}, bf16[64,512]{1,0:T(8,128)(2,1)S(1)}, u32[]{:S(2)}, u32[]{:S(2)}) %collective-permute-start.10) | collective-permute-done | bytes 65568 | tf_op jit(solution)/shard_map/ppermute | solution.py:471
  43.7 6.3 %collective-permute-done.9.refs_2_ = bf16[64,512]{1,0:T(8,128)(2,1)S(1)} collective-permute-done((bf16[64,512]{1,0:T(8,128)(2,1)S(1)}, bf16[64,512]{1,0:T(8,128)(2,1)S(1)}, u32[]{:S(2)}, u32[]{:S(2)}) %collective-permute-start.9) | collective-permute-done | bytes 65568 | tf_op jit(solution)/shard_map/ppermute | solution.py:471
  51.5 4.8 %collective-permute-done.12.refs_2_ = bf16[64,512]{1,0:T(8,128)(2,1)S(1)} collective-permute-done((bf16[64,512]{1,0:T(8,128)(2,1)S(1)}, bf16[64,512]{1,0:T(8,128)(2,1)S(1)}, u32[]{:S(2)}, u32[]{:S(2)}) %collective-permute-start.12) | collective-permute-done | bytes 65568 | tf_op jit(solution)/shard_map/ppermute | solution.py:451
  56.9 1.9 %collective-permute-done.refs_1_ = bf16[128,512]{1,0:T(8,128)(2,1)S(1)} collective-permute-done((bf16[128,512]{1,0:T(8,128)(2,1)S(1)}, bf16[128,512]{1,0:T(8,128)(2,1)S(1)}, u32[]{:S(2)}, u32[]{:S(2)}) %collective-permute-start) | collective-permute-done | bytes 131104 | tf_op jit(solution)/shard_map/ppermute | solution.py:471
  59.3 9.7 %collective-permute-done.1.refs_2_ = bf16[128,512]{1,0:T(8,128)(2,1)S(1)} collective-permute-done((bf16[128,512]{1,0:T(8,128)(2,1)S(1)}, bf16[128,512]{1,0:T(8,128)(2,1)S(1)}, u32[]{:S(2)}, u32[]{:S(2)}) %collective-permute-start.1) | collective-permute-done | bytes 131104 | tf_op jit(solution)/shard_map/ppermute | solution.py:471
  69.0 2.9 %collective-permute-start.3 = (bf16[128,512]{1,0:T(8,128)(2,1)S(1)}, bf16[128,512]{1,0:T(8,128)(2,1)S(1)}, u32[]{:S(2)}, u32[]{:S(2)}) collective-permute-start(bf16[128,512]{1,0:T(8,128)(2,1)S(1)} %get-tuple-element.27), channel_id=1, source_target_pairs={{0,16},{16,32},{32,48},{48,0},{1,17},{17,33},{33,49},{49,1},{2,18}... | collective-permute-start | bytes 393224 | tf_op jit(solution)/shard_map/ppermute | solution.py:471
  72.5 2.4 %collective-permute-done.2.refs_3_ = bf16[128,512]{1,0:T(8,128)(2,1)S(1)} collective-permute-done((bf16[128,512]{1,0:T(8,128)(2,1)S(1)}, bf16[128,512]{1,0:T(8,128)(2,1)S(1)}, u32[]{:S(2)}, u32[]{:S(2)}) %collective-permute-start.2) | collective-permute-done | bytes 131104 | tf_op jit(solution)/shard_map/ppermute | solution.py:471
  74.9 1.5 collective-permute-start.14
  76.3 1.2 collective-permute-start.18
  78.4 1.2 collective-permute-start.17
  80.3 2.3 %collective-permute-start.15 = (bf16[64,512]{1,0:T(8,128)(2,1)S(1)}, bf16[64,512]{1,0:T(8,128)(2,1)S(1)}, u32[]{:S(2)}, u32[]{:S(2)}) collective-permute-start(bf16[64,512]{1,0:T(8,128)(2,1)S(1)} %shard_map.105.refs_1_), channel_id=1, source_target_pairs={{0,4},{2,6},{4,0},{6,2},{1,5},{3,7},{5,1},{7,3},{8,12},{10,14},{12... | collective-permute-start | bytes 196616 | tf_op jit(solution)/shard_map/ppermute | solution.py:535
  82.6 15.4 %collective-permute-done.15.refs_3_ = bf16[64,512]{1,0:T(8,128)(2,1)S(1)} collective-permute-done((bf16[64,512]{1,0:T(8,128)(2,1)S(1)}, bf16[64,512]{1,0:T(8,128)(2,1)S(1)}, u32[]{:S(2)}, u32[]{:S(2)}) %collective-permute-start.15) | collective-permute-done | bytes 65568 | tf_op jit(solution)/shard_map/ppermute | solution.py:535
  98.9 3.4 %collective-permute-done.16.refs_4_ = bf16[64,512]{1,0:T(8,128)(2,1)S(1)} collective-permute-done((bf16[64,512]{1,0:T(8,128)(2,1)S(1)}, bf16[64,512]{1,0:T(8,128)(2,1)S(1)}, u32[]{:S(2)}, u32[]{:S(2)}) %collective-permute-start.16) | collective-permute-done | bytes 65568 | tf_op jit(solution)/shard_map/ppermute | solution.py:459
  102.3 2.2 %collective-permute-start.4 = (bf16[128,512]{1,0:T(8,128)(2,1)S(1)}, bf16[128,512]{1,0:T(8,128)(2,1)S(1)}, u32[]{:S(2)}, u32[]{:S(2)}) collective-permute-start(bf16[128,512]{1,0:T(8,128)(2,1)S(1)} %get-tuple-element.28), channel_id=1, source_target_pairs={{0,32},{16,48},{32,0},{48,16},{1,33},{17,49},{33,1},{49,17},{2,34}... | collective-permute-start | bytes 393224 | tf_op jit(solution)/shard_map/ppermute | solution.py:471
  105.1 6.5 %collective-permute-done.4.refs_6_ = bf16[128,512]{1,0:T(8,128)(2,1)S(1)} collective-permute-done((bf16[128,512]{1,0:T(8,128)(2,1)S(1)}, bf16[128,512]{1,0:T(8,128)(2,1)S(1)}, u32[]{:S(2)}, u32[]{:S(2)}) %collective-permute-start.4) | collective-permute-done | bytes 131104 | tf_op jit(solution)/shard_map/ppermute | solution.py:471
  111.7 2.8 %collective-permute-start.5 = (bf16[128,512]{1,0:T(8,128)(2,1)S(1)}, bf16[128,512]{1,0:T(8,128)(2,1)S(1)}, u32[]{:S(2)}, u32[]{:S(2)}) collective-permute-start(bf16[128,512]{1,0:T(8,128)(2,1)S(1)} %get-tuple-element.29), channel_id=1, source_target_pairs={{0,48},{16,0},{32,16},{48,32},{1,49},{17,1},{33,17},{49,33},{2,50}... | collective-permute-start | bytes 393224 | tf_op jit(solution)/shard_map/ppermute | solution.py:471
  114.4 11.6 %attend_first.1.refs_8_ = f32[4,512,256]{2,1,0:T(8,128)S(1)} custom-call(bf16[128,512]{1,0:T(8,128)(2,1)S(1)} %get-tuple-element.22.refs_0_, bf16[128,512]{1,0:T(8,128)(2,1)S(1)} %collective-permute-done.refs_1_, bf16[128,512]{1,0:T(8,128)(2,1)S(1)} %collective-permute-done.1.refs_2_, bf16[128,512]{1,0:T(8,128)(2,1)S(1)} %collective-permute-done.2.refs_3_, ...), custom_call_target="tpu_custom_call" | custom-call | flops 2684354560 | bytes 4194304 | tf_op jit(solution)/shard_map/attend_first/pallas_call | solution.py:243
  126.1 14.1 %attend_last.1 = (bf16[128,512]{1,0:T(8,128)(2,1)S(1)}, bf16[128,512]{1,0:T(8,128)(2,1)S(1)}, bf16[128,512]{1,0:T(8,128)(2,1)S(1)}, bf16[128,512]{1,0:T(8,128)(2,1)S(1)}, bf16[256,128]{1,0:T(8,128)(2,1)S(1)}) custom-call(bf16[128,512]{1,0:T(8,128)(2,1)S(1)} %get-tuple-element.22.refs_0_, bf16[128,512]{1,0:T(8,128)(2,1)S(1)} %collective-permute-done.refs_1_, ...), custom_call_target="tpu_custom_call" | custom-call | flops 3355443200 | bytes 4194304 | tf_op jit(solution)/shard_map/attend_last/pallas_call | solution.py:324
  140.2 9.8 %all_to_all.21.pieces_ref = bf16[8,32,128]{2,1,0:T(8,128)(2,1)S(1)} all-to-all(bf16[8,32,128]{2,1,0:T(8,128)(2,1)S(1)} %bitcast.1), channel_id=1, replica_groups=mesh['dp'=4,'zh'=4,'zl'=2,'x'=4,'y'=2] {'x','y'}, dimensions={0} | all-to-all | bytes 131072 | tf_op jit(solution)/shard_map/all_to_all | solution.py:477
  150.0 10.8 %all_to_all.22.sent_ref = bf16[8,32,128]{2,1,0:T(8,128)(2,1)S(1)} all-to-all(bf16[8,32,128]{2,1,0:T(8,128)(2,1)S(1)} %summed.1), channel_id=1, replica_groups=mesh['dp'=4,'zh'=4,'zl'=2,'x'=4,'y'=2] {'zh','zl'}, dimensions={0} | all-to-all | bytes 131072 | tf_op jit(solution)/shard_map/all_to_all | solution.py:477
  160.9 3.2 %collective-permute-start.25 = (bf16[4,32,128]{2,1,0:T(8,128)(2,1)S(1)}, bf16[4,32,128]{2,1,0:T(8,128)(2,1)S(1)}, u32[]{:S(2)}, u32[]{:S(2)}) collective-permute-start(bf16[4,32,128]{2,1,0:T(8,128)(2,1)S(1)} %pairs_summed.1.refs_0_), channel_id=1, source_target_pairs={{0,128},{64,192},{128,0},{192,64},{1,129},{65,193},{129,1},{193,65... | collective-permute-start | bytes 98312 | tf_op jit(solution)/shard_map/ppermute | solution.py:557
  164.2 2.1 %collective-permute-done.25.refs_2_ = bf16[4,32,128]{2,1,0:T(8,128)(2,1)S(1)} collective-permute-done((bf16[4,32,128]{2,1,0:T(8,128)(2,1)S(1)}, bf16[4,32,128]{2,1,0:T(8,128)(2,1)S(1)}, u32[]{:S(2)}, u32[]{:S(2)}) %collective-permute-start.25) | collective-permute-done | bytes 32800 | tf_op jit(solution)/shard_map/ppermute | solution.py:557
  166.4 2.5 %collective-permute-done.26.refs_3_ = bf16[4,32,128]{2,1,0:T(8,128)(2,1)S(1)} collective-permute-done((bf16[4,32,128]{2,1,0:T(8,128)(2,1)S(1)}, bf16[4,32,128]{2,1,0:T(8,128)(2,1)S(1)}, u32[]{:S(2)}, u32[]{:S(2)}) %collective-permute-start.26) | collective-permute-done | bytes 32800 | tf_op jit(solution)/shard_map/ppermute | solution.py:557
  168.9 1.4 route.1
  170.4 4.9 %all-to-all-start.3 = ((bf16[16,4,32,128]{3,2,1,0:T(8,128)(2,1)}), bf16[16,4,32,128]{3,2,1,0:T(8,128)(2,1)S(1)}, u32[]{:S(2)}, u32[]{:S(2)}) async-start(bf16[16,4,32,128]{3,2,1,0:T(8,128)(2,1)} %route.1), calls=%async_computation.3 | async-start | bytes 1048576 | tf_op jit(solution)/shard_map/all_to_all | solution.py:477
  175.6 3.7 %collective-permute-start.22 = (bf16[128,512]{1,0:T(8,128)(2,1)S(1)}, bf16[128,512]{1,0:T(8,128)(2,1)S(1)}, u32[]{:S(2)}, u32[]{:S(2)}) collective-permute-start(bf16[128,512]{1,0:T(8,128)(2,1)S(1)} %get-tuple-element.36), channel_id=1, source_target_pairs={{0,32},{16,48},{32,0},{48,16},{1,33},{17,49},{33,1},{49,17},{2,34}... | collective-permute-start | bytes 393224 | tf_op jit(solution)/shard_map/ppermute | solution.py:471
  179.3 10.2 %collective-permute-done.21.refs_1_ = bf16[128,512]{1,0:T(8,128)(2,1)S(1)} collective-permute-done((bf16[128,512]{1,0:T(8,128)(2,1)S(1)}, bf16[128,512]{1,0:T(8,128)(2,1)S(1)}, u32[]{:S(2)}, u32[]{:S(2)}) %collective-permute-start.21) | collective-permute-done | bytes 131104 | tf_op jit(solution)/shard_map/ppermute | solution.py:471
  (44 shorter events, 13.1 us)
Async XLA Ops:
  28.3 48.1 %collective-permute-start.6 = (bf16[8,272,128]{2,1,0:T(8,128)(2,1)S(1)}, bf16[8,272,128]{2,1,0:T(8,128)(2,1)S(1)}, u32[]{:S(2)}, u32[]{:S(2)}) collective-permute-start(bf16[8,272,128]{2,1,0:T(8,128)(2,1)S(1)} %all_to_all.20.refs_4_.refs_9_), channel_id=1, source_target_pairs={{0,1},{1,0},{2,3},{3,2},{4,5},{5,4},{6,7},{7,6},{8,9},{9,8},{10,11... | collective-permute-start | bytes 1671176 | tf_op jit(solution)/shard_map/ppermute | solution.py:451
  29.8 48.5 %collective-permute-start.7 = (bf16[8,272,128]{2,1,0:T(8,128)(2,1)S(1)}, bf16[8,272,128]{2,1,0:T(8,128)(2,1)S(1)}, u32[]{:S(2)}, u32[]{:S(2)}) collective-permute-start(bf16[8,272,128]{2,1,0:T(8,128)(2,1)S(1)} %all_to_all.20.refs_4_.refs_9_), channel_id=1, source_target_pairs={{0,2},{2,4},{4,6},{6,0},{1,3},{3,5},{5,7},{7,1},{8,10},{10,12},{12... | collective-permute-start | bytes 1671176 | tf_op jit(solution)/shard_map/ppermute | solution.py:455
  31.3 48.2 %collective-permute-start.8 = (bf16[8,272,128]{2,1,0:T(8,128)(2,1)S(1)}, bf16[8,272,128]{2,1,0:T(8,128)(2,1)S(1)}, u32[]{:S(2)}, u32[]{:S(2)}) collective-permute-start(bf16[8,272,128]{2,1,0:T(8,128)(2,1)S(1)} %all_to_all.20.refs_4_.refs_9_), channel_id=1, source_target_pairs={{0,6},{2,0},{4,2},{6,4},{1,7},{3,1},{5,3},{7,5},{8,14},{10,8},{12,... | collective-permute-start | bytes 1671176 | tf_op jit(solution)/shard_map/ppermute | solution.py:459
  31.9 0.7 copy-start
  34.7 8.4 %collective-permute-start.10 = (bf16[64,512]{1,0:T(8,128)(2,1)S(1)}, bf16[64,512]{1,0:T(8,128)(2,1)S(1)}, u32[]{:S(2)}, u32[]{:S(2)}) collective-permute-start(bf16[64,512]{1,0:T(8,128)(2,1)S(1)} %get-tuple-element.32), channel_id=1, source_target_pairs={{0,32},{16,48},{32,0},{48,16},{1,33},{17,49},{33,1},{49,17},{2,34}... | collective-permute-start | bytes 196616 | tf_op jit(solution)/shard_map/ppermute | solution.py:471
  35.4 8.3 %collective-permute-start.11 = (bf16[64,512]{1,0:T(8,128)(2,1)S(1)}, bf16[64,512]{1,0:T(8,128)(2,1)S(1)}, u32[]{:S(2)}, u32[]{:S(2)}) collective-permute-start(bf16[64,512]{1,0:T(8,128)(2,1)S(1)} %get-tuple-element.33), channel_id=1, source_target_pairs={{0,48},{16,0},{32,16},{48,32},{1,49},{17,1},{33,17},{49,33},{2,50}... | collective-permute-start | bytes 196616 | tf_op jit(solution)/shard_map/ppermute | solution.py:471
  43.2 6.8 %collective-permute-start.9 = (bf16[64,512]{1,0:T(8,128)(2,1)S(1)}, bf16[64,512]{1,0:T(8,128)(2,1)S(1)}, u32[]{:S(2)}, u32[]{:S(2)}) collective-permute-start(bf16[64,512]{1,0:T(8,128)(2,1)S(1)} %get-tuple-element.31), channel_id=1, source_target_pairs={{0,16},{16,32},{32,48},{48,0},{1,17},{17,33},{33,49},{49,1},{2,18}... | collective-permute-start | bytes 196616 | tf_op jit(solution)/shard_map/ppermute | solution.py:471
  50.6 5.7 %collective-permute-start.12 = (bf16[64,512]{1,0:T(8,128)(2,1)S(1)}, bf16[64,512]{1,0:T(8,128)(2,1)S(1)}, u32[]{:S(2)}, u32[]{:S(2)}) collective-permute-start(bf16[64,512]{1,0:T(8,128)(2,1)S(1)} %shard_map.103.refs_1_), channel_id=1, source_target_pairs={{0,8},{8,0},{1,9},{9,1},{2,10},{10,2},{3,11},{11,3},{4,12},{12,4},... | collective-permute-start | bytes 196616 | tf_op jit(solution)/shard_map/ppermute | solution.py:451
  51.5 7.3 %collective-permute-start = (bf16[128,512]{1,0:T(8,128)(2,1)S(1)}, bf16[128,512]{1,0:T(8,128)(2,1)S(1)}, u32[]{:S(2)}, u32[]{:S(2)}) collective-permute-start(bf16[128,512]{1,0:T(8,128)(2,1)S(1)} %get-tuple-element.23), channel_id=1, source_target_pairs={{0,16},{16,32},{32,48},{48,0},{1,17},{17,33},{33,49},{49,1},{2,18}... | collective-permute-start | bytes 393224 | tf_op jit(solution)/shard_map/ppermute | solution.py:471
  56.3 12.7 %collective-permute-start.1 = (bf16[128,512]{1,0:T(8,128)(2,1)S(1)}, bf16[128,512]{1,0:T(8,128)(2,1)S(1)}, u32[]{:S(2)}, u32[]{:S(2)}) collective-permute-start(bf16[128,512]{1,0:T(8,128)(2,1)S(1)} %get-tuple-element.24), channel_id=1, source_target_pairs={{0,32},{16,48},{32,0},{48,16},{1,33},{17,49},{33,1},{49,17},{2,34}... | collective-permute-start | bytes 393224 | tf_op jit(solution)/shard_map/ppermute | solution.py:471
  58.8 10.2 %collective-permute-start.13 = (bf16[64,512]{1,0:T(8,128)(2,1)S(1)}, bf16[64,512]{1,0:T(8,128)(2,1)S(1)}, u32[]{:S(2)}, u32[]{:S(2)}) collective-permute-start(bf16[64,512]{1,0:T(8,128)(2,1)S(1)} %shard_map.104.refs_1_), channel_id=1, source_target_pairs={{0,1},{1,0},{2,3},{3,2},{4,5},{5,4},{6,7},{7,6},{8,9},{9,8},{10,11... | collective-permute-start | bytes 196616 | tf_op jit(solution)/shard_map/ppermute | solution.py:451
  69.0 5.9 %collective-permute-start.2 = (bf16[128,512]{1,0:T(8,128)(2,1)S(1)}, bf16[128,512]{1,0:T(8,128)(2,1)S(1)}, u32[]{:S(2)}, u32[]{:S(2)}) collective-permute-start(bf16[128,512]{1,0:T(8,128)(2,1)S(1)} %get-tuple-element.25), channel_id=1, source_target_pairs={{0,48},{16,0},{32,16},{48,32},{1,49},{17,1},{33,17},{49,33},{2,50}... | collective-permute-start | bytes 393224 | tf_op jit(solution)/shard_map/ppermute | solution.py:471
  69.0 8.6 %collective-permute-start.3 = (bf16[128,512]{1,0:T(8,128)(2,1)S(1)}, bf16[128,512]{1,0:T(8,128)(2,1)S(1)}, u32[]{:S(2)}, u32[]{:S(2)}) collective-permute-start(bf16[128,512]{1,0:T(8,128)(2,1)S(1)} %get-tuple-element.27), channel_id=1, source_target_pairs={{0,16},{16,32},{32,48},{48,0},{1,17},{17,33},{33,49},{49,1},{2,18}... | collective-permute-start | bytes 393224 | tf_op jit(solution)/shard_map/ppermute | solution.py:471
  74.9 5.4 %collective-permute-start.14 = (bf16[64,512]{1,0:T(8,128)(2,1)S(1)}, bf16[64,512]{1,0:T(8,128)(2,1)S(1)}, u32[]{:S(2)}, u32[]{:S(2)}) collective-permute-start(bf16[64,512]{1,0:T(8,128)(2,1)S(1)} %shard_map.105.refs_1_), channel_id=1, source_target_pairs={{0,2},{2,4},{4,6},{6,0},{1,3},{3,5},{5,7},{7,1},{8,10},{10,12},{12... | collective-permute-start | bytes 196616 | tf_op jit(solution)/shard_map/ppermute | solution.py:455
  76.3 49.7 %collective-permute-start.18 = (bf16[8,272,128]{2,1,0:T(8,128)(2,1)S(1)}, bf16[8,272,128]{2,1,0:T(8,128)(2,1)S(1)}, u32[]{:S(2)}, u32[]{:S(2)}) collective-permute-start(bf16[8,272,128]{2,1,0:T(8,128)(2,1)S(1)} %collective-permute-done.6.refs_5_), channel_id=1, source_target_pairs={{0,2},{2,4},{4,6},{6,0},{1,3},{3,5},{5,7},{7,1},{8,10},{10,12},{12... | collective-permute-start | bytes 1671176 | tf_op jit(solution)/shard_map/ppermute | solution.py:455
  77.5 48.5 %collective-permute-start.19 = (bf16[8,272,128]{2,1,0:T(8,128)(2,1)S(1)}, bf16[8,272,128]{2,1,0:T(8,128)(2,1)S(1)}, u32[]{:S(2)}, u32[]{:S(2)}) collective-permute-start(bf16[8,272,128]{2,1,0:T(8,128)(2,1)S(1)} %collective-permute-done.6.refs_5_), channel_id=1, source_target_pairs={{0,6},{2,0},{4,2},{6,4},{1,7},{3,1},{5,3},{7,5},{8,14},{10,8},{12,... | collective-permute-start | bytes 1671176 | tf_op jit(solution)/shard_map/ppermute | solution.py:459
  78.4 47.7 %collective-permute-start.17 = (bf16[8,272,128]{2,1,0:T(8,128)(2,1)S(1)}, bf16[8,272,128]{2,1,0:T(8,128)(2,1)S(1)}, u32[]{:S(2)}, u32[]{:S(2)}) collective-permute-start(bf16[8,272,128]{2,1,0:T(8,128)(2,1)S(1)} %collective-permute-done.7.refs_6_), channel_id=1, source_target_pairs={{0,2},{2,4},{4,6},{6,0},{1,3},{3,5},{5,7},{7,1},{8,10},{10,12},{12... | collective-permute-start | bytes 1671176 | tf_op jit(solution)/shard_map/ppermute | solution.py:455
  79.6 46.5 %collective-permute-start.20 = (bf16[8,272,128]{2,1,0:T(8,128)(2,1)S(1)}, bf16[8,272,128]{2,1,0:T(8,128)(2,1)S(1)}, u32[]{:S(2)}, u32[]{:S(2)}) collective-permute-start(bf16[8,272,128]{2,1,0:T(8,128)(2,1)S(1)} %collective-permute-done.8.refs_7_), channel_id=1, source_target_pairs={{0,7},{1,6},{2,1},{3,0},{4,3},{5,2},{6,5},{7,4},{8,15},{9,14},{10,... | collective-permute-start | bytes 1671176 | tf_op jit(solution)/shard_map/ppermute | solution.py:464
  80.3 17.7 %collective-permute-start.15 = (bf16[64,512]{1,0:T(8,128)(2,1)S(1)}, bf16[64,512]{1,0:T(8,128)(2,1)S(1)}, u32[]{:S(2)}, u32[]{:S(2)}) collective-permute-start(bf16[64,512]{1,0:T(8,128)(2,1)S(1)} %shard_map.105.refs_1_), channel_id=1, source_target_pairs={{0,4},{2,6},{4,0},{6,2},{1,5},{3,7},{5,1},{7,3},{8,12},{10,14},{12... | collective-permute-start | bytes 196616 | tf_op jit(solution)/shard_map/ppermute | solution.py:535
  98.0 4.3 %collective-permute-start.16 = (bf16[64,512]{1,0:T(8,128)(2,1)S(1)}, bf16[64,512]{1,0:T(8,128)(2,1)S(1)}, u32[]{:S(2)}, u32[]{:S(2)}) collective-permute-start(bf16[64,512]{1,0:T(8,128)(2,1)S(1)} %shard_map.105.refs_1_), channel_id=1, source_target_pairs={{0,6},{2,0},{4,2},{6,4},{1,7},{3,1},{5,3},{7,5},{8,14},{10,8},{12,... | collective-permute-start | bytes 196616 | tf_op jit(solution)/shard_map/ppermute | solution.py:459
  102.3 9.4 %collective-permute-start.4 = (bf16[128,512]{1,0:T(8,128)(2,1)S(1)}, bf16[128,512]{1,0:T(8,128)(2,1)S(1)}, u32[]{:S(2)}, u32[]{:S(2)}) collective-permute-start(bf16[128,512]{1,0:T(8,128)(2,1)S(1)} %get-tuple-element.28), channel_id=1, source_target_pairs={{0,32},{16,48},{32,0},{48,16},{1,33},{17,49},{33,1},{49,17},{2,34}... | collective-permute-start | bytes 393224 | tf_op jit(solution)/shard_map/ppermute | solution.py:471
  111.7 14.3 %collective-permute-start.5 = (bf16[128,512]{1,0:T(8,128)(2,1)S(1)}, bf16[128,512]{1,0:T(8,128)(2,1)S(1)}, u32[]{:S(2)}, u32[]{:S(2)}) collective-permute-start(bf16[128,512]{1,0:T(8,128)(2,1)S(1)} %get-tuple-element.29), channel_id=1, source_target_pairs={{0,48},{16,0},{32,16},{48,32},{1,49},{17,1},{33,17},{49,33},{2,50}... | collective-permute-start | bytes 393224 | tf_op jit(solution)/shard_map/ppermute | solution.py:471
  126.1 42.9 %copy-start.1 = (s32[4]{0:T(128)S(1)}, s32[4]{0:T(128)}, u32[]{:S(2)}) copy-start(s32[4]{0:T(128)} %tasks_ref.3) | copy-start | bytes 52
  160.8 3.5 %collective-permute-start.24 = (bf16[4,32,128]{2,1,0:T(8,128)(2,1)S(1)}, bf16[4,32,128]{2,1,0:T(8,128)(2,1)S(1)}, u32[]{:S(2)}, u32[]{:S(2)}) collective-permute-start(bf16[4,32,128]{2,1,0:T(8,128)(2,1)S(1)} %pairs_summed.1.refs_0_), channel_id=1, source_target_pairs={{0,64},{64,0},{128,192},{192,128},{1,65},{65,1},{129,193},{193,129... | collective-permute-start | bytes 98312 | tf_op jit(solution)/shard_map/ppermute | solution.py:557
  160.9 5.5 %collective-permute-start.25 = (bf16[4,32,128]{2,1,0:T(8,128)(2,1)S(1)}, bf16[4,32,128]{2,1,0:T(8,128)(2,1)S(1)}, u32[]{:S(2)}, u32[]{:S(2)}) collective-permute-start(bf16[4,32,128]{2,1,0:T(8,128)(2,1)S(1)} %pairs_summed.1.refs_0_), channel_id=1, source_target_pairs={{0,128},{64,192},{128,0},{192,64},{1,129},{65,193},{129,1},{193,65... | collective-permute-start | bytes 98312 | tf_op jit(solution)/shard_map/ppermute | solution.py:557
  164.0 4.9 %collective-permute-start.26 = (bf16[4,32,128]{2,1,0:T(8,128)(2,1)S(1)}, bf16[4,32,128]{2,1,0:T(8,128)(2,1)S(1)}, u32[]{:S(2)}, u32[]{:S(2)}) collective-permute-start(bf16[4,32,128]{2,1,0:T(8,128)(2,1)S(1)} %pairs_summed.1.refs_0_), channel_id=1, source_target_pairs={{0,192},{64,128},{128,64},{192,0},{1,193},{65,129},{129,65},{193,1... | collective-permute-start | bytes 98312 | tf_op jit(solution)/shard_map/ppermute | solution.py:557
  170.4 20.9 %all-to-all-start.3 = ((bf16[16,4,32,128]{3,2,1,0:T(8,128)(2,1)}), bf16[16,4,32,128]{3,2,1,0:T(8,128)(2,1)S(1)}, u32[]{:S(2)}, u32[]{:S(2)}) async-start(bf16[16,4,32,128]{3,2,1,0:T(8,128)(2,1)} %route.1), calls=%async_computation.3 | async-start | bytes 1048576 | tf_op jit(solution)/shard_map/all_to_all | solution.py:477
  175.2 14.3 %collective-permute-start.21 = (bf16[128,512]{1,0:T(8,128)(2,1)S(1)}, bf16[128,512]{1,0:T(8,128)(2,1)S(1)}, u32[]{:S(2)}, u32[]{:S(2)}) collective-permute-start(bf16[128,512]{1,0:T(8,128)(2,1)S(1)} %get-tuple-element.35), channel_id=1, source_target_pairs={{0,48},{16,0},{32,16},{48,32},{1,49},{17,1},{33,17},{49,33},{2,50}... | collective-permute-start | bytes 393224 | tf_op jit(solution)/shard_map/ppermute | solution.py:471
  175.6 13.9 %collective-permute-start.22 = (bf16[128,512]{1,0:T(8,128)(2,1)S(1)}, bf16[128,512]{1,0:T(8,128)(2,1)S(1)}, u32[]{:S(2)}, u32[]{:S(2)}) collective-permute-start(bf16[128,512]{1,0:T(8,128)(2,1)S(1)} %get-tuple-element.36), channel_id=1, source_target_pairs={{0,32},{16,48},{32,0},{48,16},{1,33},{17,49},{33,1},{49,17},{2,34}... | collective-permute-start | bytes 393224 | tf_op jit(solution)/shard_map/ppermute | solution.py:471
  179.3 11.1 %collective-permute-start.23 = (bf16[128,512]{1,0:T(8,128)(2,1)S(1)}, bf16[128,512]{1,0:T(8,128)(2,1)S(1)}, u32[]{:S(2)}, u32[]{:S(2)}) collective-permute-start(bf16[128,512]{1,0:T(8,128)(2,1)S(1)} %get-tuple-element.37), channel_id=1, source_target_pairs={{0,16},{16,32},{32,48},{48,0},{1,17},{17,33},{33,49},{49,1},{2,18}... | collective-permute-start | bytes 393224 | tf_op jit(solution)/shard_map/ppermute | solution.py:471
